TPU v7x, 32 devices: a whole 2x2x4 slice. The times are simulated.
32 devices in a mesh: wide: 8 (over z, x), narrow: 4 (over y, core).
Axes of the slice: x: 2, y: 2, z: 4, core: 2. Of those that a mesh axis runs over, the one named last changes fastest.
Arguments:
- tokens: bfloat16 [4096, 1024], P(('wide', 'narrow')), may hold values from -6 to 6
- cotangent: bfloat16 [4096, 1024], P(('wide', 'narrow')), may hold values from -0.0625 to 0.0625
- segment_ids: int32 [32, 128], P(('wide', 'narrow')), may hold values from 0 to 7, never falling along the last dimension, each value on 1 to 32 neighbouring positions
- w_qkv: float32 [1024, 3072], P(('wide', 'narrow')), may hold values from -0.1875 to 0.1875
- w_out: float32 [1024, 1024], P(('wide', 'narrow')), may hold values from -0.375 to 0.375
- w_up: float32 [1024, 4096], P(('wide', 'narrow')), may hold values from -0.1875 to 0.1875
- w_down: float32 [4096, 1024], P(('wide', 'narrow')), may hold values from -0.09375 to 0.09375
- vectors: float32 [1024, 12], P(('wide', 'narrow')), as said below
- moments_qkv: float32 [2, 1024, 3072], P(None, ('wide', 'narrow')), as said below
- moments_out: float32 [2, 1024, 1024], P(None, ('wide', 'narrow')), as said below
- moments_up: float32 [2, 1024, 4096], P(None, ('wide', 'narrow')), as said below
- moments_down: float32 [2, 4096, 1024], P(None, ('wide', 'narrow')), as said below
- moments_vec: float32 [2, 1024, 12], P(None, ('wide', 'narrow')), as said below
Outputs:
- block_out: bfloat16 [4096, 1024], P(('wide', 'narrow'))
- input_grad: float32 [4096, 1024], P(('wide', 'narrow'))
- new_qkv: float32 [1024, 3072], P(('wide', 'narrow'))
- new_out: float32 [1024, 1024], P(('wide', 'narrow'))
- new_up: float32 [1024, 4096], P(('wide', 'narrow'))
- new_down: float32 [4096, 1024], P(('wide', 'narrow'))
- new_vectors: float32 [1024, 12], P(('wide', 'narrow'))
- state_qkv: float32 [2, 1024, 3072], P(None, ('wide', 'narrow'))
- state_out: float32 [2, 1024, 1024], P(None, ('wide', 'narrow'))
- state_up: float32 [2, 1024, 4096], P(None, ('wide', 'narrow'))
- state_down: float32 [2, 4096, 1024], P(None, ('wide', 'narrow'))
- state_vectors: float32 [2, 1024, 12], P(None, ('wide', 'narrow'))
- copy_qkv: bfloat16 [1024, 3072], P(('wide', 'narrow'))
- copy_out: bfloat16 [1024, 1024], P(('wide', 'narrow'))
- copy_up: bfloat16 [1024, 4096], P(('wide', 'narrow'))
- copy_down: bfloat16 [4096, 1024], P(('wide', 'narrow'))
- copy_vectors: bfloat16 [1024, 12], P(('wide', 'narrow'))
Inputs may be any that keep to these rules, and one draw needn't show every extreme that they name: `segment_ids`: in each sequence the ids never fall, every id is used, each segment has 1 to 32 patches and one has exactly 32. `vectors`: columns 0 and 5 are positive gains; the others are biases of both signs. `moments_qkv`: the second slice is positive. `moments_out`: the second slice is positive. `moments_up`: the second slice is positive. `moments_down`: the second slice is positive. `moments_vec`: the second slice is positive.
All inputs are finite; a program needn't handle non-finite values.
Results may differ from a plain program's by a relative error of at most 0.02.
Values may be sent and summed in bfloat16 or wider, within the bound.
A program may use at most 256 MiB of HBM per device.

v0:
```python
import jax
import jax.numpy as jnp
from jax import lax
from jax.sharding import PartitionSpec as P

D = 1024
HEADS = 16
FF = 4096
STEP = 3


NORM_EPSILON = 1e-06
MASK_VALUE = -1e30
MOMENT_DECAY = 0.5
RATE_MATRIX = 0.04
RATE_VECTOR = 0.2
WEIGHT_DECAY = 0.1
ADAM_EPSILON = 1e-08


def layer_norm(values, scale_row, offset_row):
    center = values - jnp.mean(values, axis=-1, keepdims=True)
    spread = jnp.mean(center * center, axis=-1, keepdims=True)
    return center * lax.rsqrt(spread + NORM_EPSILON) * scale_row + offset_row


def exact_gelu(values):
    return jax.nn.gelu(values, approximate=False)


def adam_update(master, moments, gradient, rate, decay):
    first_moment = MOMENT_DECAY * moments[0] + (1.0 - MOMENT_DECAY) * gradient
    second_moment = MOMENT_DECAY * moments[1] + (1.0 - MOMENT_DECAY) * gradient * gradient
    correction = 1.0 - MOMENT_DECAY**STEP
    normalized = first_moment / correction / (jnp.sqrt(second_moment / correction) + ADAM_EPSILON)
    updated = master - rate * (normalized + decay * master)
    return (updated, jnp.stack([first_moment, second_moment]), updated.astype(jnp.bfloat16))


def unpack_vectors(packed):
    columns = [packed[:, column] for column in range(8)]
    columns.append(packed[:, 8:].T.reshape(FF))
    return columns


def body(
    tokens,
    cotangent,
    segment_ids,
    w_qkv,
    w_out,
    w_up,
    w_down,
    vectors,
    moments_qkv,
    moments_out,
    moments_up,
    moments_down,
    moments_vec,
):
    qkv_low = w_qkv.astype(jnp.bfloat16)
    out_low = w_out.astype(jnp.bfloat16)
    up_low = w_up.astype(jnp.bfloat16)
    down_low = w_down.astype(jnp.bfloat16)
    vec_low = vectors.astype(jnp.bfloat16)
    gathered = (
        lax.all_gather(qkv_low, ("wide", "narrow"), axis=0, tiled=True),
        lax.all_gather(out_low, ("wide", "narrow"), axis=0, tiled=True),
        lax.all_gather(up_low, ("wide", "narrow"), axis=0, tiled=True),
        lax.all_gather(down_low, ("wide", "narrow"), axis=0, tiled=True),
        lax.all_gather(vec_low, ("wide", "narrow"), axis=0, tiled=True),
    )
    qkv_full, out_full, up_full, down_full, vec_full = gathered
    length = tokens.shape[0]
    block_rows = min(512, length)
    block_count = length // block_rows
    head_dim = D // HEADS
    scale_value = head_dim ** (-0.5)
    segments = segment_ids[0]
    (
        gain_one,
        shift_one,
        bias_query,
        bias_value,
        bias_out,
        gain_two,
        shift_two,
        bias_down,
        bias_up,
    ) = unpack_vectors(vec_full.astype(jnp.float32))
    inputs = tokens.astype(jnp.float32)
    normed_one = layer_norm(inputs, gain_one, shift_one).astype(jnp.bfloat16)
    qkv_bias = jnp.concatenate([bias_query, jnp.zeros_like(bias_query), bias_value])
    qkv_value = (
        jnp.dot(normed_one, qkv_full, preferred_element_type=jnp.float32) + qkv_bias
    ).astype(jnp.bfloat16)
    queries = qkv_value[:, :D].reshape(length, HEADS, head_dim)
    keys_all = qkv_value[:, D : 2 * D].reshape(length, HEADS, head_dim)
    values_all = qkv_value[:, 2 * D :].reshape(length, HEADS, head_dim)
    query_blocks = queries.reshape(block_count, block_rows, HEADS, head_dim)
    segment_blocks = segments.reshape(block_count, block_rows)

    def masked_scores(query_block, segment_block):
        raw_scores = (
            jnp.einsum("qhd,khd->hqk", query_block, keys_all, preferred_element_type=jnp.float32)
            * scale_value
        )
        same_segment = segment_block[:, None] == segments[None, :]
        return jnp.where(same_segment[None], raw_scores, MASK_VALUE)

    def attend(pieces):
        query_block, segment_block = pieces
        scores = masked_scores(query_block, segment_block)
        highest = jnp.max(scores, axis=-1, keepdims=True)
        exp_scores = jnp.exp(scores - highest)
        totals = jnp.sum(exp_scores, axis=-1, keepdims=True)
        soft_weights = (exp_scores / totals).astype(jnp.bfloat16)
        mixed = jnp.einsum(
            "hqk,khd->qhd", soft_weights, values_all, preferred_element_type=jnp.float32
        )
        return (mixed.astype(jnp.bfloat16), (highest + jnp.log(totals))[:, :, 0])

    attended, log_totals = lax.map(attend, (query_blocks, segment_blocks))
    attended = attended.reshape(length, D)
    resid_one = inputs + jnp.dot(attended, out_full, preferred_element_type=jnp.float32) + bias_out
    normed_two = layer_norm(resid_one, gain_two, shift_two).astype(jnp.bfloat16)
    hidden_pre = jnp.dot(normed_two, up_full, preferred_element_type=jnp.float32) + bias_up
    hidden_act, gelu_pull = jax.vjp(exact_gelu, hidden_pre)
    hidden_low = hidden_act.astype(jnp.bfloat16)
    block_out = (
        resid_one + jnp.dot(hidden_low, down_full, preferred_element_type=jnp.float32) + bias_down
    ).astype(jnp.bfloat16)
    back_weights = (
        lax.all_gather(qkv_low, ("wide", "narrow"), axis=0, tiled=True),
        lax.all_gather(out_low, ("wide", "narrow"), axis=0, tiled=True),
        lax.all_gather(up_low, ("wide", "narrow"), axis=0, tiled=True),
        lax.all_gather(down_low, ("wide", "narrow"), axis=0, tiled=True),
        lax.all_gather(vec_low, ("wide", "narrow"), axis=0, tiled=True),
    )
    qkv_back, out_back, up_back, down_back, vec_back = back_weights
    back_params = unpack_vectors(vec_back.astype(jnp.float32))
    grad_down = jnp.einsum("sf,sd->fd", hidden_low, cotangent, preferred_element_type=jnp.float32)
    grad_bias_down = jnp.sum(cotangent.astype(jnp.float32), axis=0)
    grad_hidden = jnp.einsum("sd,fd->sf", cotangent, down_back, preferred_element_type=jnp.float32)
    grad_pre = gelu_pull(grad_hidden)[0].astype(jnp.bfloat16)
    grad_up = jnp.einsum("sd,sf->df", normed_two, grad_pre, preferred_element_type=jnp.float32)
    grad_bias_up = jnp.sum(grad_pre.astype(jnp.float32), axis=0)
    grad_normed_two = jnp.einsum("sf,df->sd", grad_pre, up_back, preferred_element_type=jnp.float32)
    norm_value_two, norm_pull_two = jax.vjp(layer_norm, resid_one, back_params[5], back_params[6])
    part_resid, grad_gain_two, grad_shift_two = norm_pull_two(grad_normed_two)
    grad_resid = cotangent.astype(jnp.float32) + part_resid
    grad_branch = grad_resid.astype(jnp.bfloat16)
    grad_out = jnp.einsum("sd,se->de", attended, grad_branch, preferred_element_type=jnp.float32)
    grad_bias_out = jnp.sum(grad_resid, axis=0)
    grad_attended = jnp.einsum(
        "se,de->sd", grad_branch, out_back, preferred_element_type=jnp.float32
    ).astype(jnp.bfloat16)
    grad_blocks = grad_attended.reshape(block_count, block_rows, HEADS, head_dim)

    def attend_back(running, pieces):
        key_grad, value_grad = running
        query_block, segment_block, grad_block, log_block = pieces
        scores = masked_scores(query_block, segment_block)
        soft_weights = jnp.exp(scores - log_block[:, :, None])
        value_grad = value_grad + jnp.einsum(
            "hqk,qhd->khd",
            soft_weights.astype(jnp.bfloat16),
            grad_block,
            preferred_element_type=jnp.float32,
        )
        grad_soft = jnp.einsum(
            "qhd,khd->hqk", grad_block, values_all, preferred_element_type=jnp.float32
        )
        inner_sum = jnp.sum(soft_weights * grad_soft, axis=-1, keepdims=True)
        grad_scores = (soft_weights * (grad_soft - inner_sum)).astype(jnp.bfloat16)
        query_grad = (
            jnp.einsum("hqk,khd->qhd", grad_scores, keys_all, preferred_element_type=jnp.float32)
            * scale_value
        )
        key_grad = (
            key_grad
            + jnp.einsum(
                "hqk,qhd->khd", grad_scores, query_block, preferred_element_type=jnp.float32
            )
            * scale_value
        )
        return ((key_grad, value_grad), query_grad)

    zero_heads = jnp.zeros((length, HEADS, head_dim), jnp.float32)
    (key_grad, value_grad), query_grad = lax.scan(
        attend_back,
        (zero_heads, zero_heads),
        (query_blocks, segment_blocks, grad_blocks, log_totals),
    )
    grad_qkv = jnp.concatenate(
        [query_grad.reshape(length, D), key_grad.reshape(length, D), value_grad.reshape(length, D)],
        axis=1,
    ).astype(jnp.bfloat16)
    grad_qkv_weight = jnp.einsum(
        "sd,sf->df", normed_one, grad_qkv, preferred_element_type=jnp.float32
    )
    qkv_sums = jnp.sum(grad_qkv.astype(jnp.float32), axis=0)
    grad_normed_one = jnp.einsum(
        "sf,df->sd", grad_qkv, qkv_back, preferred_element_type=jnp.float32
    )
    norm_value_one, norm_pull_one = jax.vjp(layer_norm, inputs, back_params[0], back_params[1])
    part_input, grad_gain_one, grad_shift_one = norm_pull_one(grad_normed_one)
    input_grad = grad_resid + part_input
    vector_head = jnp.stack(
        [
            grad_gain_one,
            grad_shift_one,
            qkv_sums[:D],
            qkv_sums[2 * D :],
            grad_bias_out,
            grad_gain_two,
            grad_shift_two,
            grad_bias_down,
        ],
        axis=1,
    )
    vector_grad = jnp.concatenate([vector_head, grad_bias_up.reshape(FF // D, D).T], axis=1)
    wide_count = lax.axis_size("wide")
    narrow_count = lax.axis_size("narrow")

    def split_rows(gradient):
        return gradient.reshape(
            wide_count,
            narrow_count,
            gradient.shape[0] // (wide_count * narrow_count),
            gradient.shape[1],
        )

    group_sums = (
        lax.psum_scatter(
            split_rows(grad_qkv_weight).astype(jnp.bfloat16),
            "narrow",
            scatter_dimension=1,
            tiled=True,
        ).astype(jnp.float32),
        lax.psum_scatter(
            split_rows(grad_out).astype(jnp.bfloat16), "narrow", scatter_dimension=1, tiled=True
        ).astype(jnp.float32),
        lax.psum_scatter(
            split_rows(grad_up).astype(jnp.bfloat16), "narrow", scatter_dimension=1, tiled=True
        ).astype(jnp.float32),
        lax.psum_scatter(
            split_rows(grad_down).astype(jnp.bfloat16), "narrow", scatter_dimension=1, tiled=True
        ).astype(jnp.float32),
        lax.psum_scatter(
            split_rows(vector_grad).astype(jnp.bfloat16), "narrow", scatter_dimension=1, tiled=True
        ).astype(jnp.float32),
    )
    owned_sums = (
        lax.psum_scatter(
            group_sums[0].astype(jnp.bfloat16), "wide", scatter_dimension=0, tiled=True
        ).astype(jnp.float32),
        lax.psum_scatter(
            group_sums[1].astype(jnp.bfloat16), "wide", scatter_dimension=0, tiled=True
        ).astype(jnp.float32),
        lax.psum_scatter(
            group_sums[2].astype(jnp.bfloat16), "wide", scatter_dimension=0, tiled=True
        ).astype(jnp.float32),
        lax.psum_scatter(
            group_sums[3].astype(jnp.bfloat16), "wide", scatter_dimension=0, tiled=True
        ).astype(jnp.float32),
        lax.psum_scatter(
            group_sums[4].astype(jnp.bfloat16), "wide", scatter_dimension=0, tiled=True
        ).astype(jnp.float32),
    )
    reduced = tuple((member.reshape(member.shape[2], member.shape[3]) for member in owned_sums))
    new_qkv, state_qkv, copy_qkv = adam_update(
        w_qkv, moments_qkv, reduced[0], RATE_MATRIX, WEIGHT_DECAY
    )
    new_out, state_out, copy_out = adam_update(
        w_out, moments_out, reduced[1], RATE_MATRIX, WEIGHT_DECAY
    )
    new_up, state_up, copy_up = adam_update(w_up, moments_up, reduced[2], RATE_MATRIX, WEIGHT_DECAY)
    new_down, state_down, copy_down = adam_update(
        w_down, moments_down, reduced[3], RATE_MATRIX, WEIGHT_DECAY
    )
    new_vectors, state_vectors, copy_vectors = adam_update(
        vectors, moments_vec, reduced[4], RATE_VECTOR, 0.0
    )
    return (
        block_out,
        input_grad,
        new_qkv,
        new_out,
        new_up,
        new_down,
        new_vectors,
        state_qkv,
        state_out,
        state_up,
        state_down,
        state_vectors,
        copy_qkv,
        copy_out,
        copy_up,
        copy_down,
        copy_vectors,
    )


def solution(mesh):
    placed = (
        P(("wide", "narrow"), None),
        P(("wide", "narrow"), None),
        P(("wide", "narrow"), None),
        P(("wide", "narrow"), None),
        P(("wide", "narrow"), None),
        P(("wide", "narrow"), None),
        P(("wide", "narrow"), None),
        P(("wide", "narrow"), None),
        P(None, ("wide", "narrow"), None),
        P(None, ("wide", "narrow"), None),
        P(None, ("wide", "narrow"), None),
        P(None, ("wide", "narrow"), None),
        P(None, ("wide", "narrow"), None),
    )
    return jax.shard_map(
        body,
        mesh=mesh,
        in_specs=placed,
        out_specs=(
            P(("wide", "narrow"), None),
            P(("wide", "narrow"), None),
            P(("wide", "narrow"), None),
            P(("wide", "narrow"), None),
            P(("wide", "narrow"), None),
            P(("wide", "narrow"), None),
            P(("wide", "narrow"), None),
            P(None, ("wide", "narrow"), None),
            P(None, ("wide", "narrow"), None),
            P(None, ("wide", "narrow"), None),
            P(None, ("wide", "narrow"), None),
            P(None, ("wide", "narrow"), None),
            P(("wide", "narrow"), None),
            P(("wide", "narrow"), None),
            P(("wide", "narrow"), None),
            P(("wide", "narrow"), None),
            P(("wide", "narrow"), None),
        ),
        check_vma=False,
    )
```

profile of v0, /device:TPU:0, one launch (start us, length us, event | category | flops | bytes accessed | tf_op | source)
XLA Modules:
  0.0 1126.8 jit_solution(3805992562656520872)
XLA Ops:
  7.3 1.8 convert_element_type.142
  9.1 1.5 convert_element_type.147
  10.7 1.8 convert_element_type.149
  12.6 0.7 convert_element_type.151
  13.6 43.8 %all-gather = bf16[32,32,12]{1,2,0:T(8,128)(2,1)S(1)} all-gather(bf16[1,32,12]{1,2,0:T(8,128)(2,1)S(1)} %convert_bitcast_fusion.10), channel_id=1, replica_groups=mesh['wide'=8,'narrow'=4] {'wide','narrow'}, dimensions={0}, use_global_device_ids=true | all-gather | bytes 25344 | tf_op jit(solution)/shard_map/all_gather | solution.py:71
  58.1 25.6 %all-gather.6.cloned.1.call-done = bf16[1024,3072]{1,0:T(8,128)(2,1)} async-done(((bf16[32,3072]{1,0:T(8,128)(2,1)}), bf16[1024,3072]{1,0:T(8,128)(2,1)}) %all-gather.6.cloned.1.call-update) | async-done | bytes 6291472 | tf_op jit(solution)/shard_map/all_gather | solution.py:67
  83.7 3.9 fusion
  88.2 0.4 fusion.109
  88.7 0.3 convolution_convert_fusion.6
  89.1 52.9 %all-gather.8.cloned.1.call-done = bf16[1024,1024]{1,0:T(8,128)(2,1)} async-done(((bf16[32,1024]{1,0:T(8,128)(2,1)}), bf16[1024,1024]{1,0:T(8,128)(2,1)}) %all-gather.8.cloned.1.call-update) | async-done | bytes 2097168 | tf_op jit(solution)/shard_map/all_gather | solution.py:68
  141.9 2.1 fusion.110
  144.3 77.0 %all-gather.10.cloned.1.call-done = bf16[1024,4096]{1,0:T(8,128)(2,1)} async-done(((bf16[32,4096]{1,0:T(8,128)(2,1)}), bf16[1024,4096]{1,0:T(8,128)(2,1)}) %all-gather.10.cloned.1.call-update) | async-done | bytes 8388624 | tf_op jit(solution)/shard_map/all_gather | solution.py:69
  221.3 6.1 convolution_add_fusion
  227.4 72.9 %all-gather.12.cloned.1.call-done = bf16[4096,1024]{1,0:T(8,128)(2,1)} async-done(((bf16[128,1024]{1,0:T(8,128)(2,1)}), bf16[4096,1024]{1,0:T(8,128)(2,1)}) %all-gather.12.cloned.1.call-update) | async-done | bytes 8388624 | tf_op jit(solution)/shard_map/all_gather | solution.py:70
  300.3 10.9 fusion.102
  311.2 3.0 multiply_reduce_fusion.1
  314.2 0.3 fusion.104
  314.5 0.8 convolution_convert_fusion.5
  315.6 0.5 convolution_convert_fusion.4
  316.0 1.3 multiply_reduce_fusion
  317.6 0.5 fusion.12
  318.1 0.2 copy-done.11
  318.3 0.3 fusion.11
  318.6 0.3 fusion.87
  318.9 4.7 convolution_convert_fusion.2
  323.6 5.7 convolution_convert_fusion.1
  329.8 5.1 fusion.91
  334.9 0.4 fusion.23
  335.2 1.1 fusion.90
  336.9 0.7 copy.95
  337.6 0.3 all-reduce.7.cloned.1.call-start
  337.9 5.6 convolution_convert_fusion
  343.4 2.1 convolution_convert_fusion.3
  345.6 0.6 copy-done.28
  346.2 0.6 dynamic-slice
  346.8 9.2 reduce-scatter.27.cloned.1.call-done
  356.0 1.4 copy.96
  357.4 424.2 %all-reduce.7.cloned.1.call-done = (bf16[8,4,32,3072]{3,2,1,0:T(8,128)(2,1)}, bf16[8,4,32,1024]{3,2,1,0:T(8,128)(2,1)}, bf16[8,4,32,4096]{3,2,1,0:T(8,128)(2,1)}, bf16[8,4,128,1024]{3,2,1,0:T(8,128)(2,1)}) async-done(((bf16[8,4,32,3072]{3,2,1,0:T(8,128)(2,1)}, bf16[8,4,32,1024]{3,2,1,0:T(8,128)(2,1)}, bf16[8,4,32,4096]{3,2,1,0:T(8,128)(2,1)}, bf16[8,4,128,1024]{3,2,1,0:T(8,128)(2,1)}), ...) | async-done | bytes 25165840
  781.6 2.5 constant_dynamic-slice_fusion.2
  784.2 3.3 constant_dynamic-slice_fusion.3
  787.6 3.8 constant_dynamic-slice_fusion.1
  791.5 0.6 copy-done.26
  792.1 5.4 fusion.10
  797.5 3.8 constant_dynamic-slice_fusion
  801.3 39.0 %reduce-scatter.29.cloned.1.call-done = bf16[1,1,32,12]{2,3,1,0:T(8,128)(2,1)} async-done(((bf16[8,1,32,12]{2,3,1,0:T(8,128)(2,1)}), bf16[1,1,32,12]{2,3,1,0:T(8,128)(2,1)}) %reduce-scatter.29.cloned.1.call-update) | async-done | bytes 784 | tf_op jit(solution)/shard_map/reduce_scatter | solution.py:267
  840.3 0.7 multiply_add_fusion.8
  841.0 0.6 copy.100
  841.6 1.3 fusion.92
  842.9 63.0 %reduce-scatter.21.cloned.1.call-done = bf16[1,1,32,1024]{3,2,1,0:T(8,128)(2,1)} async-done(((bf16[8,1,32,1024]{3,2,1,0:T(8,128)(2,1)}), bf16[1,1,32,1024]{3,2,1,0:T(8,128)(2,1)}) %reduce-scatter.21.cloned.1.call-update) | async-done | bytes 65552 | tf_op jit(solution)/shard_map/reduce_scatter | solution.py:258
  905.9 0.9 multiply_add_fusion.6
  906.7 0.7 pad_maximum_fusion.4
  907.5 1.7 fusion.98
  909.2 64.7 %reduce-scatter.19.cloned.1.call-done = bf16[1,1,32,3072]{3,2,1,0:T(8,128)(2,1)} async-done(((bf16[8,1,32,3072]{3,2,1,0:T(8,128)(2,1)}), bf16[1,1,32,3072]{3,2,1,0:T(8,128)(2,1)}) %reduce-scatter.19.cloned.1.call-update) | async-done | bytes 196624 | tf_op jit(solution)/shard_map/reduce_scatter | solution.py:255
  973.8 1.1 multiply_add_fusion.4
  975.0 0.9 pad_maximum_fusion.3
  975.9 1.1 fusion.100
  977.0 67.6 %reduce-scatter.23.cloned.1.call-done = bf16[1,1,32,4096]{3,2,1,0:T(8,128)(2,1)} async-done(((bf16[8,1,32,4096]{3,2,1,0:T(8,128)(2,1)}), bf16[1,1,32,4096]{3,2,1,0:T(8,128)(2,1)}) %reduce-scatter.23.cloned.1.call-update) | async-done | bytes 262160 | tf_op jit(solution)/shard_map/reduce_scatter | solution.py:261
  1044.6 1.1 multiply_add_fusion.1
  1045.7 1.0 pad_maximum_fusion
  1046.7 68.8 %reduce-scatter.25.cloned.1.call-done = bf16[1,1,128,1024]{3,2,1,0:T(8,128)(2,1)} async-done(((bf16[8,1,128,1024]{3,2,1,0:T(8,128)(2,1)}), bf16[1,1,128,1024]{3,2,1,0:T(8,128)(2,1)}) %reduce-scatter.25.cloned.1.call-update) | async-done | bytes 262160 | tf_op jit(solution)/shard_map/reduce_scatter | solution.py:264
  1115.5 1.1 multiply_add_fusion
  1116.6 1.1 pad_maximum_fusion.1
  1117.7 1.3 fusion.96
  1119.0 1.3 fusion.94
  (128 shorter events, 3.9 us)
Async XLA Ops:
  7.2 5.4 copy-start.13
  7.2 6.2 copy-start.4
  7.2 6.4 copy-start.25
  7.2 50.4 %copy-start.1 = (bf16[128,1024]{1,0:T(8,128)(2,1)S(1)}, bf16[128,1024]{1,0:T(8,128)(2,1)}, u32[]{:S(2)}) copy-start(bf16[128,1024]{1,0:T(8,128)(2,1)} %param.13) | copy-start | bytes 786436
  7.2 76.4 %all-gather.6.cloned.1.call-start = ((), (), s32[]{:S(2)}) async-start(), calls=%async_computation.6 | async-start | bytes 6488064 | tf_op jit(solution)/shard_map/all_gather | solution.py:67
  9.0 48.9 %copy-start.27 = (s32[1,128]{1,0:T(1,128)S(1)}, s32[1,128]{1,0:T(1,128)}, u32[]{:S(2)}) copy-start(s32[1,128]{1,0:T(1,128)} %param.15) | copy-start | bytes 1540
  9.1 132.8 %all-gather.8.cloned.1.call-start = ((), (), s32[]{:S(2)}) async-start(), calls=%async_computation.7 | async-start | bytes 2162688 | tf_op jit(solution)/shard_map/all_gather | solution.py:68
  10.7 210.6 %all-gather.10.cloned.1.call-start = ((), (), s32[]{:S(2)}) async-start(), calls=%async_computation.8 | async-start | bytes 8650752 | tf_op jit(solution)/shard_map/all_gather | solution.py:69
  12.5 287.8 %all-gather.12.cloned.1.call-start = ((), (), s32[]{:S(2)}) async-start(), calls=%async_computation.9 | async-start | bytes 8650752 | tf_op jit(solution)/shard_map/all_gather | solution.py:70
  13.4 342.6 %reduce-scatter.27.cloned.1.call-start = ((), (), s32[]{:S(2)}) async-start(), calls=%async_computation.14 | async-start | bytes 122880 | tf_op jit(solution)/shard_map/reduce_scatter | solution.py:250
  87.8 1.2 copy-start.10
  88.2 0.9 copy-start.19
  89.0 138.3 %copy-start.21 = (bf16[16,64,128]{2,1,0:T(8,128)(2,1)}, bf16[16,64,128]{2,1,0:T(8,128)(2,1)S(1)}, u32[]{:S(2)}) copy-start(bf16[16,64,128]{2,1,0:T(8,128)(2,1)S(1)} %convolution_convert_fusion.6) | copy-start | bytes 786436
  300.3 10.9 copy-start
  311.2 3.0 copy-start.5
  311.2 3.3 copy-start.3
  317.4 1.0 copy-start.11
  318.9 4.7 copy-start.6
  323.6 5.7 copy-start.2
  323.6 5.7 copy-start.15
  337.6 5.9 copy-start.22
  337.6 444.0 %all-reduce.7.cloned.1.call-start = ((), (), s32[]{:S(2)}) async-start(), calls=%async_computation.16 | async-start | bytes 50331648
  345.6 0.7 copy-start.28
  345.6 494.7 %reduce-scatter.29.cloned.1.call-start = ((), (), s32[]{:S(2)}) async-start(), calls=%async_computation.15 | async-start | bytes 36864 | tf_op jit(solution)/shard_map/reduce_scatter | solution.py:267
  357.4 548.5 %reduce-scatter.21.cloned.1.call-start = ((), (), s32[]{:S(2)}) async-start(), calls=%async_computation.11 | async-start | bytes 589824 | tf_op jit(solution)/shard_map/reduce_scatter | solution.py:258
  784.1 189.7 %reduce-scatter.19.cloned.1.call-start = ((), (), s32[]{:S(2)}) async-start(), calls=%async_computation.10 | async-start | bytes 1769472 | tf_op jit(solution)/shard_map/reduce_scatter | solution.py:255
  787.5 257.1 %reduce-scatter.23.cloned.1.call-start = ((), (), s32[]{:S(2)}) async-start(), calls=%async_computation.12 | async-start | bytes 2359296 | tf_op jit(solution)/shard_map/reduce_scatter | solution.py:261
  791.4 0.7 copy-start.26
  791.4 324.1 %reduce-scatter.25.cloned.1.call-start = ((), (), s32[]{:S(2)}) async-start(), calls=%async_computation.13 | async-start | bytes 2359296 | tf_op jit(solution)/shard_map/reduce_scatter | solution.py:264
  801.2 104.6 %copy-start.20 = (f32[2,32,1024]{2,1,0:T(8,128)S(1)}, f32[2,32,1024]{2,1,0:T(8,128)}, u32[]{:S(2)}) copy-start(f32[2,32,1024]{2,1,0:T(8,128)} %param.22) | copy-start | bytes 786436
  801.2 106.3 %copy-start.24 = (f32[32,1024]{1,0:T(8,128)S(1)}, f32[32,1024]{1,0:T(8,128)}, u32[]{:S(2)}) copy-start(f32[32,1024]{1,0:T(8,128)} %param.17) | copy-start | bytes 393220
  801.2 172.6 %copy-start.9 = (f32[2,32,3072]{2,1,0:T(8,128)S(1)}, f32[2,32,3072]{2,1,0:T(8,128)}, u32[]{:S(2)}) copy-start(f32[2,32,3072]{2,1,0:T(8,128)} %param.21) | copy-start | bytes 2359300
  907.5 68.4 %copy-start.16 = (f32[32,3072]{1,0:T(8,128)S(1)}, f32[32,3072]{1,0:T(8,128)}, u32[]{:S(2)}) copy-start(f32[32,3072]{1,0:T(8,128)} %param.16) | copy-start | bytes 1179652
  973.8 2.0 copy-start.23
  974.9 69.7 %copy-start.7 = (f32[2,32,4096]{2,1,0:T(8,128)S(1)}, f32[2,32,4096]{2,1,0:T(8,128)}, u32[]{:S(2)}) copy-start(f32[2,32,4096]{2,1,0:T(8,128)} %param.23) | copy-start | bytes 3145732
  977.0 138.5 %copy-start.8 = (f32[2,128,1024]{2,1,0:T(8,128)S(1)}, f32[2,128,1024]{2,1,0:T(8,128)}, u32[]{:S(2)}) copy-start(f32[2,128,1024]{2,1,0:T(8,128)} %param.24) | copy-start | bytes 3145732
  1046.7 71.0 %copy-start.12 = (f32[32,4096]{1,0:T(8,128)S(1)}, f32[32,4096]{1,0:T(8,128)}, u32[]{:S(2)}) copy-start(f32[32,4096]{1,0:T(8,128)} %param.18) | copy-start | bytes 1572868
  1046.7 71.0 %copy-start.17 = (bf16[1,1,32,4096]{3,2,1,0:T(8,128)(2,1)S(1)}, bf16[1,1,32,4096]{3,2,1,0:T(8,128)(2,1)}, u32[]{:S(2)}) copy-start(bf16[1,1,32,4096]{3,2,1,0:T(8,128)(2,1)} %reduce-scatter.23.cloned.1.call-done) | copy-start | bytes 786436
  1116.6 2.4 copy-start.14
  1116.6 2.4 copy-start.18
Sparse Core Ops, SparseCore 0:
  11.5 72.1 all-gather.5
  87.1 54.7 all-gather.7
  145.4 75.9 all-gather.9
  224.6 75.6 all-gather.11
  337.7 18.2 reduce-scatter.26
  358.6 422.9 all-reduce.6
  785.3 54.9 reduce-scatter.28
  844.2 61.6 reduce-scatter.20
  909.3 64.4 reduce-scatter.18
  977.2 67.3 reduce-scatter.22
  1048.1 67.3 reduce-scatter.24
where the time goes:
time: 1130 us
  waiting for transfers between devices  965 us (85%)
  matrix products  58.5 us (5%)
  blocking collectives  43.8 us (4%)
  other arithmetic  24.5 us (2%)
  local copies, waits for them, and re-layouts  19.9 us (2%)
  between operations  14.4 us (1%)
    unnamed x12, waiting for transfers between devices  424 us
    all_gather x1, waiting for transfers between devices, body(): lax.all_gather(up_low, ('wide', 'narrow'), axis=0, tiled=True)  77 us
    all_gather x1, waiting for transfers between devices, body(): lax.all_gather(down_low, ('wide', 'narrow'), axis=0, tiled=True)  72.9 us
    reduce_scatter x1, waiting for transfers between devices, body(): lax.psum_scatter(group_sums[3].astype(jnp.bfloat16), 'wide', scatter_dime...  68.8 us
    reduce_scatter x1, waiting for transfers between devices, body(): lax.psum_scatter(group_sums[2].astype(jnp.bfloat16), 'wide', scatter_dime...  67.6 us
    reduce_scatter x1, waiting for transfers between devices, body(): lax.psum_scatter(group_sums[0].astype(jnp.bfloat16), 'wide', scatter_dime...  64.7 us
    reduce_scatter x1, waiting for transfers between devices, body(): lax.psum_scatter(group_sums[1].astype(jnp.bfloat16), 'wide', scatter_dime...  63 us
    all_gather x1, waiting for transfers between devices, body(): lax.all_gather(out_low, ('wide', 'narrow'), axis=0, tiled=True)  52.9 us
  transfers between devices with their start and end apart: 11, of which 11 were waited for; matrix products, arithmetic and copies ran while one was open for 5% of the time, Pallas kernels for 0%

commit v1 on v0

v1 whole, which is shorter than its diff:
```python
import types

import jax
import jax.numpy as jnp
from jax import lax
from jax.experimental import pallas as pl
from jax.experimental.pallas import tpu as pltpu
from jax.sharding import PartitionSpec as P

D = 1024
HEADS = 16
FF = 4096
STEP = 3
HEAD = D // HEADS

NORM_EPSILON = 1e-06
MASK_VALUE = -1e30
MOMENT_DECAY = 0.5
RATE_MATRIX = 0.04
RATE_VECTOR = 0.2
WEIGHT_DECAY = 0.1
ADAM_EPSILON = 1e-08

BF = jnp.bfloat16
F32 = jnp.float32
MESH = pl.DeviceIdType.MESH


def adam_update(master, moments, gradient, rate, decay):
    first_moment = MOMENT_DECAY * moments[0] + (1.0 - MOMENT_DECAY) * gradient
    second_moment = MOMENT_DECAY * moments[1] + (1.0 - MOMENT_DECAY) * gradient * gradient
    correction = 1.0 - MOMENT_DECAY**STEP
    normalized = first_moment / correction / (jnp.sqrt(second_moment / correction) + ADAM_EPSILON)
    updated = master - rate * (normalized + decay * master)
    return (updated, jnp.stack([first_moment, second_moment]), updated.astype(BF))


def nn(left, right):
    return jnp.dot(left, right, preferred_element_type=F32)


def nt(left, right):
    return lax.dot_general(left, right, (((1,), (1,)), ((), ())), preferred_element_type=F32)


def tn(left, right):
    return lax.dot_general(left, right, (((0,), (0,)), ((), ())), preferred_element_type=F32)


def loop(count, body):
    def step(index, carry):
        body(index)
        return carry

    lax.fori_loop(0, count, step, 0)


def normalize(rows):
    center = rows - jnp.mean(rows, axis=-1, keepdims=True)
    inverse = lax.rsqrt(jnp.mean(center * center, axis=-1, keepdims=True) + NORM_EPSILON)
    return center * inverse, inverse


def norm_back(grad, unit, inverse, gain):
    scaled = grad * gain
    first = jnp.mean(scaled, axis=-1, keepdims=True)
    second = jnp.mean(scaled * unit, axis=-1, keepdims=True)
    return inverse * (scaled - first - unit * second)


def layout(wide, narrow, length):
    m = types.SimpleNamespace()
    m.W, m.T, m.S = wide, narrow, length
    m.Y = narrow // 2
    m.X = narrow // 2
    m.Z = wide // m.X
    m.L = length * narrow
    m.Q = D // narrow
    m.NQ = 3 * m.Q
    m.F = FF // narrow
    m.RG = D // wide
    m.RD = D // (wide * narrow)
    m.FD = FF // (wide * narrow)
    m.NH = m.Q // HEAD
    m.inside = m.RD % 16 == 0
    return m


def scratch_of(m):
    def weights(name, rows, cols):
        return {
            name: ((m.W, rows, cols), BF),
        }

    def scatter(name, rows, cols):
        return {
            "G" + name: ((m.W, rows, cols), BF),
            "X" + name: ((m.X - 1, m.Z, rows, cols), BF),
            "S" + name: ((m.Z, rows, cols), BF),
            "Z" + name: ((m.Z - 1, rows, cols), BF),
        }

    def spread(name, cols):
        return {
            "T" + name: ((m.T, m.RD, cols), BF),
            "N" + name: ((m.T, m.RD, cols), BF),
        }

    def partial(name):
        return {
            "P" + name: ((m.L, D), BF),
            "C" + name: ((m.Y, m.S, D), BF),
            "M" + name: ((m.Y, m.S, D), BF),
            "A" + name: ((m.S, D), F32),
            "R" + name: ((m.Y - 1, m.S, D), BF),
        }

    out = {}
    out.update(weights("wq", m.RG, m.NQ))
    out["wo"] = ((m.T, m.W, m.RG, m.Q), BF)
    out.update(weights("wu", m.RG, m.F))
    out.update(weights("wd", m.FD, D))
    out.update(weights("wv", 16, D))
    out["vn"] = ((m.T - 1, 16, D), BF)
    out.update(scatter("q", m.RG, m.NQ))
    out.update(scatter("o", m.RG, m.Q))
    out.update(scatter("u", m.RG, m.F))
    out.update(scatter("d", m.FD, D))
    if m.inside:
        out.update(spread("q", m.NQ))
        out.update(spread("o", m.Q))
        out.update(spread("u", m.F))
    for name in ("y", "c", "n"):
        out.update(partial(name))
    for name in ("tok", "dya", "ca"):
        out[name] = ((m.L, D), BF)
    out["oa"] = ((m.T, m.L, m.Q), BF)
    out["sg"] = ((m.T, 8, m.S), F32)
    out["vec"] = ((16, D), F32)
    out["bias"] = ((8, m.NQ), F32)
    out["a"] = ((m.L, D), BF)
    out["at"] = ((D, m.L), BF)
    out["ct"] = ((D, m.L), BF)
    out["ot"] = ((D, m.L), BF)
    out["h"] = ((m.L, m.F), BF)
    out["ht"] = ((m.F, m.L), BF)
    out["u"] = ((m.L, m.F), F32)
    out["du"] = ((m.L, m.F), BF)
    out["qkv"] = ((m.L, m.NQ), BF)
    out["dqkv"] = ((m.L, m.NQ), BF)
    out["prob"] = ((m.T * m.NH, m.S, m.S), F32)
    out["oo"] = ((m.S, D), BF)
    out["r1"] = ((m.S, D), F32)
    out["dr"] = ((m.S, D), F32)
    out["da"] = ((m.S, D), BF)
    out["dob"] = ((m.T, m.S, m.Q), BF)
    out["dab"] = ((m.T, m.S, m.Q), BF)
    out["dof"] = ((m.L, m.Q), BF)
    out["daq"] = ((m.L, m.Q), BF)
    out["sums"] = ((6, 16, D), F32)
    out["vg"] = ((3, 16, D), F32)
    out["vx"] = ((m.X - 1, 16, D), F32)
    out["vz"] = ((m.Z - 1, 16, D), F32)
    out["vt"] = ((m.T - 1, 16, D), F32)
    return out


def semaphores_of(m):
    gather = (m.Z - 1) + m.Z * (m.X - 1)
    scatter = m.Z * (m.X - 1) + (m.Z - 1)
    pair = (m.Y - 1) + m.Y
    direct = m.T - 1
    total = 5 * gather + 4 * scatter + 8 * pair + 10 * direct + (m.X - 1) + (m.Z - 1) + direct
    return 2 * total + 16


def block_kernel(m, names, *refs):
    inputs = ("x", "dy", "seg", "pq", "po", "pu", "pd", "pv")
    outputs = ("bo", "ig", "gq", "go", "gu", "gd", "gv")
    r = types.SimpleNamespace(**dict(zip(inputs + outputs + tuple(names) + ("sem",), refs)))
    w, n = lax.axis_index("wide"), lax.axis_index("narrow")
    z, x = w // m.X, lax.rem(w, m.X)
    y, c = n // 2, lax.rem(n, 2)
    sibling = (w, 2 * y + 1 - c)
    L, S, T, X, Y, Z = m.L, m.S, m.T, m.X, m.Y, m.Z
    sent = []
    used = [0]

    def fresh(count):
        first = used[0]
        used[0] += count
        return [first + k for k in range(count)]

    def copy(src, dst, device, index):
        return pltpu.make_async_remote_copy(
            src_ref=src,
            dst_ref=dst,
            send_sem=r.sem.at[2 * index],
            recv_sem=r.sem.at[2 * index + 1],
            device_id=device,
            device_id_type=MESH,
        )

    def send(src, dst, device, index):
        one = copy(src, dst, device, index)
        one.start()
        sent.append(one)

    def arrive(dst, index):
        copy(dst, dst, sibling, index).wait_recv()

    def up_z(step):
        return lax.rem(z + step, Z)

    def down_z(step):
        return lax.rem(z + Z - step, Z)

    def up_x(step):
        return lax.rem(x + step, X)

    def down_x(step):
        return lax.rem(x + X - step, X)

    def up_n(step):
        return lax.rem(n + step, T)

    def down_n(step):
        return lax.rem(n + T - step, T)

    def at_y(step):
        return lax.rem(y + Y + step, Y)

    def rows_of(index, size):
        return pl.ds(pl.multiple_of(index * size, size), size)

    class Gather:
        def __init__(self, ref):
            self.ref = ref
            self.zi = fresh(Z - 1)
            self.xi = fresh(Z * (X - 1))

        def along_z(self):
            for step in range(1, Z):
                send(self.ref.at[w], self.ref.at[w], (up_z(step) * X + x, n), self.zi[step - 1])

        def forward(self, step):
            block = down_z(step) * X + x if step else w
            for dx in range(1, X):
                send(
                    self.ref.at[block],
                    self.ref.at[block],
                    (z * X + up_x(dx), n),
                    self.xi[step * (X - 1) + dx - 1],
                )

        def relay(self, step):
            arrive(self.ref.at[down_z(step) * X + x], self.zi[step - 1])
            self.forward(step)

        def relays(self):
            for step in range(1, Z):
                self.relay(step)

        def finish(self):
            for step in range(Z):
                for dx in range(1, X):
                    block = (down_z(step) if step else z) * X + down_x(dx)
                    arrive(self.ref.at[block], self.xi[step * (X - 1) + dx - 1])

    class Share:
        def __init__(self, slot):
            self.slot = slot
            self.yi = fresh(Y - 1)
            self.ci = fresh(Y)

        def start(self):
            for step in range(1, Y):
                send(self.slot(n), self.slot(n), (w, 2 * at_y(step) + c), self.yi[step - 1])
            send(self.slot(n), self.slot(n), sibling, self.ci[0])

        def middle(self):
            for step in range(1, Y):
                block = 2 * at_y(-step) + c
                arrive(self.slot(block), self.yi[step - 1])
                send(self.slot(block), self.slot(block), sibling, self.ci[step])

        def finish(self):
            self.middle()
            for step in range(Y):
                block = 2 * at_y(-step) + 1 - c
                arrive(self.slot(block), self.ci[step])

    class Total:
        def __init__(self, name):
            self.part = getattr(r, "P" + name)
            self.core = getattr(r, "C" + name)
            self.mid = getattr(r, "M" + name)
            self.own = getattr(r, "A" + name)
            self.last = getattr(r, "R" + name)
            self.yi = fresh(Y - 1)
            self.ci = fresh(Y)

        def start(self):
            for step in list(range(1, Y)) + [0]:
                block = 2 * at_y(step) + 1 - c
                send(self.part.at[rows_of(block, S)], self.core.at[step], sibling, self.ci[step])

        def middle(self):
            for step in list(range(1, Y)) + [0]:
                block = 2 * at_y(step) + c
                arrive(self.core.at[step], self.ci[step])

                def add(i):
                    rows = rows_of(i, 16)
                    mine = self.part[pl.ds(pl.multiple_of(block * S + i * 16, 16), 16), :]
                    total = mine.astype(F32) + self.core[step, rows, :].astype(F32)
                    if step:
                        self.mid[step, rows, :] = total.astype(BF)
                    else:
                        self.own[rows, :] = total

                loop(S // 16, add)
                if step:
                    send(self.mid.at[step], self.last.at[step - 1], (w, block), self.yi[step - 1])

        def finish(self):
            for step in range(1, Y):
                arrive(self.last.at[step - 1], self.yi[step - 1])

        def rows(self, rows):
            total = self.own[rows, :]
            for step in range(1, Y):
                total = total + self.last[step - 1, rows, :].astype(F32)
            return total

    class Scatter:
        def __init__(self, name, rows, cols):
            self.rows, self.cols = rows, cols
            self.grad = getattr(r, "G" + name)
            self.fromx = getattr(r, "X" + name)
            self.sums = getattr(r, "S" + name)
            self.fromz = getattr(r, "Z" + name)
            self.xi = fresh(Z * (X - 1))
            self.zi = fresh(Z - 1)
            self.chunk = 16 if cols > 512 else 32
            if rows % self.chunk:
                self.chunk = 16

        def order(self):
            return list(range(1, Z)) + [0]

        def multiply(self, step, left, right):
            first = up_z(step) if step else z
            high = X * self.rows
            tile = 256 if self.cols % 256 == 0 else 128

            def one(j):
                cols = rows_of(j, tile)
                value = nn(left[rows_of(first, high), :], right[:, cols]).astype(BF)
                value = value.reshape(X, self.rows, tile)
                self.grad[rows_of(first, X), :, cols] = value

            loop(self.cols // tile, one)

        def along_x(self, step):
            first = up_z(step) if step else z
            for dx in range(1, X):
                other = up_x(dx)
                send(
                    self.grad.at[first * X + other],
                    self.fromx.at[dx - 1, step],
                    (z * X + other, n),
                    self.xi[step * (X - 1) + dx - 1],
                )

        def along_z(self, step):
            block = (up_z(step) if step else z) * X + x
            for dx in range(1, X):
                arrive(self.fromx.at[dx - 1, step], self.xi[step * (X - 1) + dx - 1])

            def add(i):
                rows = rows_of(i, self.chunk)
                total = self.grad[block, rows, :].astype(F32)
                for dx in range(1, X):
                    total = total + self.fromx[dx - 1, step, rows, :].astype(F32)
                self.sums[step, rows, :] = total.astype(BF)

            loop(self.rows // self.chunk, add)
            if step:
                send(self.sums.at[step], self.fromz.at[step - 1], (block, n), self.zi[step - 1])

        def finish(self):
            for step in range(1, Z):
                arrive(self.fromz.at[step - 1], self.zi[step - 1])

        def total(self, rows):
            total = self.sums[0, rows, :].astype(F32)
            for step in range(1, Z):
                total = total + self.fromz[step - 1, rows, :].astype(F32)
            return total

    class Deal:
        def __init__(self, name, scatter, out):
            self.scatter, self.out = scatter, out
            if m.inside:
                self.turn = getattr(r, "T" + name)
                self.got = getattr(r, "N" + name)
                self.ni = fresh(T - 1)

        def start(self):
            self.scatter.finish()
            if not m.inside:
                def store(i):
                    rows = rows_of(i, self.scatter.chunk)
                    self.out[rows, :] = self.scatter.total(rows).astype(BF)

                loop(self.scatter.rows // self.scatter.chunk, store)
                return

            def add(i):
                self.turn[i] = self.scatter.total(rows_of(i, m.RD)).astype(BF)

            loop(T, add)
            for step in range(1, T):
                other = up_n(step)
                send(self.turn.at[other], self.got.at[step], (w, other), self.ni[step - 1])

        def finish(self):
            if not m.inside:
                return
            self.out[n] = self.turn[n]
            for step in range(1, T):
                arrive(self.got.at[step], self.ni[step - 1])
                self.out[down_n(step)] = self.got[step]

    def transpose(target, source, count_rows, count_cols):
        def tile(k):
            i, j = k // count_cols, lax.rem(k, count_cols)
            value = source(rows_of(i, 128), rows_of(j, 128)).astype(F32)
            target[rows_of(j, 128), rows_of(i, 128)] = value.T.astype(BF)

        loop(count_rows * count_cols, tile)

    barrier = pltpu.get_barrier_semaphore()
    peers = [(w, up_n(k)) for k in range(1, T)]
    peers += [(up_z(k) * X + x, n) for k in range(1, Z)]
    peers += [(z * X + up_x(k), n) for k in range(1, X)]
    for peer in peers:
        pl.semaphore_signal(barrier, inc=1, device_id=peer, device_id_type=MESH)
    pl.semaphore_wait(barrier, len(peers))

    gv, gq, gu, gd = Gather(r.wv), Gather(r.wq), Gather(r.wu), Gather(r.wd)
    go = Gather(r.wo.at[n])
    tokens = Share(lambda k: r.tok.at[rows_of(k, S)])
    cotangents = Share(lambda k: r.dya.at[rows_of(k, S)])
    outs = Share(lambda k: r.wo.at[k])
    mixes = Share(lambda k: r.oa.at[k])
    seconds = Share(lambda k: r.ca.at[rows_of(k, S)])
    ty, tc, tin = Total("y"), Total("c"), Total("n")
    sd, su = Scatter("d", m.FD, D), Scatter("u", m.RG, m.F)
    so, sq = Scatter("o", m.RG, m.Q), Scatter("q", m.RG, m.NQ)

    vi, si = fresh(T - 1), fresh(T - 1)
    r.sg[n] = r.seg[...]
    for step in range(1, T):
        send(r.pv, r.vn.at[step - 1], (w, up_n(step)), vi[step - 1])
    shares = []
    if m.inside:
        for part, target in ((r.po, None), (r.pq, r.wq), (r.pu, r.wu)):
            ids = fresh(T - 1)
            own = pl.ds(pl.multiple_of(n * m.RD, m.RD), m.RD)
            for step in range(1, T):
                other = up_n(step)
                there = r.wo.at[other, w, own] if target is None else target.at[w, own]
                send(part.at[other], there, (w, other), ids[step - 1])
            shares.append((target, ids))
            if target is None:
                r.wo[n, w, own, :] = part[n]
            else:
                target[w, own, :] = part[n]
    else:
        r.wo[n, w] = r.po[...]
        r.wq[w] = r.pq[...]
        r.wu[w] = r.pu[...]
    r.wd[w] = r.pd[...]
    own_rows = rows_of(n, S)
    r.tok[own_rows, :] = r.x[...]
    r.dya[own_rows, :] = r.dy[...]
    for step in range(1, T):
        send(r.sg.at[n], r.sg.at[n], (w, up_n(step)), si[step - 1])
    tokens.start()
    cotangents.start()

    vector = r.pv[...].astype(F32)
    for step in range(1, T):
        arrive(r.vn.at[step - 1], vi[step - 1])
        vector = vector + r.vn[step - 1].astype(F32)
    r.wv[w] = vector.astype(BF)
    gv.along_z()
    gv.forward(0)

    def shared(k):
        if m.inside:
            target, ids = shares[k]
            for step in range(1, T):
                got = pl.ds(pl.multiple_of(down_n(step) * m.RD, m.RD), m.RD)
                arrive(r.wo.at[n, w, got] if target is None else target.at[w, got], ids[step - 1])

    shared(0)
    go.along_z()
    go.forward(0)
    shared(1)
    gq.along_z()
    shared(2)
    gu.along_z()
    gd.along_z()
    gv.relays()
    go.relays()
    gq.forward(0)
    tokens.finish()
    gv.finish()
    vector = r.wv[0].astype(F32)
    for k in range(1, m.W):
        vector = vector + r.wv[k].astype(F32)
    r.vec[...] = vector

    heads = rows_of(n, m.Q)
    r.bias[...] = jnp.zeros_like(r.bias)
    r.bias[0:1, 0 : m.Q] = r.vec[2:3, heads]
    r.bias[0:1, 2 * m.Q : 3 * m.Q] = r.vec[3:4, heads]

    def first_norm(i):
        rows = rows_of(i, 16)
        unit, _ = normalize(r.tok[rows, :].astype(F32))
        r.a[rows, :] = (unit * r.vec[0:1, :] + r.vec[1:2, :]).astype(BF)

    loop(L // 16, first_norm)
    cotangents.finish()
    go.finish()
    outs.start()
    transpose(r.at, lambda i, j: r.a[i, j], L // 128, D // 128)
    gq.relays()
    gu.forward(0)
    outs.middle()
    gq.finish()

    tile_q = 256 if m.NQ % 256 == 0 else 128

    def project(j):
        cols = rows_of(j, tile_q)
        value = nn(r.a[...], r.wq[:, :, cols].reshape(D, tile_q)) + r.bias[0:1, cols]
        r.qkv[:, cols] = value.astype(BF)

    loop(m.NQ // tile_q, project)
    for step in range(1, T):
        arrive(r.sg.at[down_n(step)], si[step - 1])

    lane = lax.broadcasted_iota(jnp.int32, (1, 128), 1)
    halves = [(lane // HEAD == k).astype(F32) for k in range(128 // HEAD)]
    scale = HEAD ** (-0.5)
    per = 128 // HEAD

    def pick(values):
        total = values[0] * halves[0]
        for k in range(1, per):
            total = total + values[k] * halves[k]
        return total

    def attend(s):
        rows = rows_of(s, S)
        keys = jnp.broadcast_to(r.sg[s, 0:1, :], (S, S))
        same = keys == keys.T
        for pair in range(m.Q // 128):
            q = r.qkv[rows, pair * 128 : pair * 128 + 128]
            k = r.qkv[rows, m.Q + pair * 128 : m.Q + pair * 128 + 128]
            v = r.qkv[rows, 2 * m.Q + pair * 128 : 2 * m.Q + pair * 128 + 128]
            mixed = []
            for half in range(per):
                score = nt(q * halves[half].astype(BF), k) * scale
                score = jnp.where(same, score, MASK_VALUE)
                power = jnp.exp(score - jnp.max(score, axis=-1, keepdims=True))
                weight = power / jnp.sum(power, axis=-1, keepdims=True)
                r.prob[s * m.NH + pair * per + half] = weight
                mixed.append(nn(weight.astype(BF), v))
            r.oa[n, rows, pair * 128 : pair * 128 + 128] = pick(mixed).astype(BF)

    loop(T, attend)
    mixes.start()
    gu.relay(1)
    for k in range(2, Z - 1):
        gu.relay(k)
    mixes.middle()
    for step in range(Y):
        arrive(outs.slot(2 * at_y(-step) + 1 - c), outs.ci[step])
    for step in range(Y):
        arrive(mixes.slot(2 * at_y(-step) + 1 - c), mixes.ci[step])

    for t in range(T):
        r.oo[:, t * m.Q : (t + 1) * m.Q] = r.oa[t, own_rows, :]
    for t in range(T):
        cols = slice(t * m.Q, (t + 1) * m.Q)
        value = nn(r.oo[...], r.wo[t].reshape(D, m.Q))
        r.r1[:, cols] = r.x[:, cols].astype(F32) + value + r.vec[4:5, cols]

    def second_norm(i):
        rows = rows_of(i, 16)
        unit, _ = normalize(r.r1[rows, :])
        there = pl.ds(pl.multiple_of(n * S + i * 16, 16), 16)
        r.ca[there, :] = (unit * r.vec[5:6, :] + r.vec[6:7, :]).astype(BF)

    loop(S // 16, second_norm)
    seconds.start()
    gu.relay(Z - 1)
    gd.forward(0)
    seconds.middle()
    for t in range(T):
        for k in range(m.Q // 128):
            base = t * m.Q + k * 128

            def turn(i, t=t, k=k, base=base):
                value = r.oa[t, rows_of(i, 128), k * 128 : k * 128 + 128].astype(F32)
                r.ot[base : base + 128, rows_of(i, 128)] = value.T.astype(BF)

            loop(L // 128, turn)
    for step in range(Y):
        arrive(seconds.slot(2 * at_y(-step) + 1 - c), seconds.ci[step])
    transpose(r.ct, lambda i, j: r.ca[i, j], L // 128, D // 128)
    gu.finish()

    def expand(j):
        cols = rows_of(j, 256)
        value = nn(r.ca[...], r.wu[:, :, cols].reshape(D, 256))
        r.u[:, cols] = value + r.vec[pl.ds(8 + n, 1), cols]

    loop(m.F // 256, expand)

    def activate(i):
        rows = rows_of(i, 16)
        value = r.u[rows, :]
        phi = 0.5 * (1.0 + lax.erf(value * (0.5**0.5)))
        r.h[rows, :] = (value * phi).astype(BF)
        r.u[rows, :] = phi + value * (jnp.exp(-0.5 * value * value) * 0.3989422804014327)

    loop(L // 16, activate)
    transpose(r.ht, lambda i, j: r.h[i, j], L // 128, m.F // 128)
    for step in sd.order():
        sd.multiply(step, r.ht, r.dya)
    gd.relays()
    for step in sd.order():
        sd.along_x(step)
    gd.finish()

    group = 256 // m.FD

    def expand_back(j):
        cols = rows_of(j, 256)
        value = nt(r.dya[...], r.wd[rows_of(j, group)].reshape(256, D)) * r.u[:, cols]
        low = value.astype(BF)
        r.du[:, cols] = low
        r.sums[5, 0:1, cols] = jnp.sum(low.astype(F32), axis=0, keepdims=True)

    loop(m.F // 256, expand_back)
    width = 256 // m.RG

    def up_back(j):
        value = nt(r.du[...], r.wu[rows_of(j, width)].reshape(256, m.F))
        r.Pc[:, rows_of(j, 256)] = value.astype(BF)

    loop(D // 256, up_back)
    tc.start()
    for step in su.order():
        su.multiply(step, r.ct, r.du)
        su.along_x(step)
    tc.middle()

    def contract(j):
        cols = rows_of(j, 256)
        r.Py[:, cols] = nn(r.h[...], r.wd[:, :, cols].reshape(m.F, 256)).astype(BF)

    loop(D // 256, contract)
    sd.along_z(1)
    tc.finish()
    r.sums[0:4] = jnp.zeros((4, 16, D), F32)

    def second_back(i):
        rows = rows_of(i, 16)
        grad = tc.rows(rows)
        cot = r.dy[rows, :].astype(F32)
        unit, inverse = normalize(r.r1[rows, :])
        total = cot + norm_back(grad, unit, inverse, r.vec[5:6, :])
        r.dr[rows, :] = total
        r.da[rows, :] = total.astype(BF)
        r.sums[0] += total
        r.sums[1] += grad * unit
        r.sums[2] += grad
        r.sums[3] += cot

    loop(S // 16, second_back)
    oi, ai = fresh(T - 1), fresh(T - 1)
    share = m.Q // m.RG
    for step in list(range(1, T)) + [0]:
        other = up_n(step) if step else n
        value = jnp.zeros((S, m.Q), F32)
        for t in range(T):
            block = r.wo[t, rows_of(other, share)].reshape(m.Q, m.Q)
            value = value + nt(r.da[:, t * m.Q : (t + 1) * m.Q], block)
        if step:
            r.dob[step] = value.astype(BF)
            send(r.dob.at[step], r.dof.at[own_rows], (w, other), oi[step - 1])
        else:
            r.dof[own_rows, :] = value.astype(BF)
    for step in range(1, T):
        other = up_n(step)
        r.dab[step] = r.da[:, rows_of(other, m.Q)]
        send(r.dab.at[step], r.daq.at[own_rows], (w, other), ai[step - 1])
    r.daq[own_rows, :] = r.da[:, rows_of(n, m.Q)]
    ty.start()
    sd.along_z(2 if Z > 2 else 0)
    for step in range(1, T):
        arrive(r.dof.at[rows_of(down_n(step), S)], oi[step - 1])

    def attend_back(s):
        rows = rows_of(s, S)
        for pair in range(m.Q // 128):
            at = [pl.ds(b * m.Q + pair * 128, 128) for b in range(3)]
            q, k, v = r.qkv[rows, at[0]], r.qkv[rows, at[1]], r.qkv[rows, at[2]]
            cot = r.dof[rows, pair * 128 : pair * 128 + 128]
            dq, dk, dv = [], [], []
            for half in range(per):
                weight = r.prob[s * m.NH + pair * per + half]
                grad = nt(cot * halves[half].astype(BF), v)
                inner = jnp.sum(weight * grad, axis=-1, keepdims=True)
                ds = (weight * (grad - inner)).astype(BF)
                dq.append(nn(ds, k))
                dk.append(tn(ds, q))
                dv.append(tn(weight.astype(BF), cot))
            r.dqkv[rows, at[0]] = (pick(dq) * scale).astype(BF)
            r.dqkv[rows, at[1]] = (pick(dk) * scale).astype(BF)
            r.dqkv[rows, at[2]] = pick(dv).astype(BF)

    loop(T, attend_back)

    def project_back(j):
        value = nt(r.dqkv[...], r.wq[rows_of(j, width)].reshape(256, m.NQ))
        r.Pn[:, rows_of(j, 256)] = value.astype(BF)

    loop(D // 256, project_back)
    tin.start()
    for step in range(1, T):
        arrive(r.daq.at[rows_of(down_n(step), S)], ai[step - 1])
    for step in so.order():
        so.multiply(step, r.ot, r.daq)
        so.along_x(step)
    tin.middle()
    for step in sq.order():
        sq.multiply(step, r.at, r.dqkv)
        sq.along_x(step)
    for step in sd.order()[2:]:
        sd.along_z(step)

    r.vg[0] = jnp.zeros((16, D), F32)
    for k, row in enumerate((4, 5, 6, 7)):
        r.vg[0, row : row + 1, :] = jnp.sum(r.sums[k], axis=0, keepdims=True)
    r.vg[0, pl.ds(8 + n, 1), 0 : m.F] = r.sums[5, 0:1, 0 : m.F]

    def column(j):
        cols = rows_of(j, 128)
        there = pl.ds(pl.multiple_of(n * m.Q + j * 128, 128), 128)
        tail = pl.ds(pl.multiple_of(2 * m.Q + j * 128, 128), 128)
        r.vg[0, 2:3, there] = jnp.sum(r.dqkv[:, cols].astype(F32), axis=0, keepdims=True)
        r.vg[0, 3:4, there] = jnp.sum(r.dqkv[:, tail].astype(F32), axis=0, keepdims=True)

    loop(m.Q // 128, column)
    tin.finish()
    r.sums[0:2] = jnp.zeros((2, 16, D), F32)

    def first_back(i):
        rows = rows_of(i, 16)
        grad = tin.rows(rows)
        unit, inverse = normalize(r.x[rows, :].astype(F32))
        r.ig[rows, :] = r.dr[rows, :] + norm_back(grad, unit, inverse, r.vec[0:1, :])
        r.sums[0] += grad * unit
        r.sums[1] += grad

    loop(S // 16, first_back)
    r.vg[0, 0:1, :] = jnp.sum(r.sums[0], axis=0, keepdims=True)
    r.vg[0, 1:2, :] = jnp.sum(r.sums[1], axis=0, keepdims=True)
    vxi, vzi, vti = fresh(X - 1), fresh(Z - 1), fresh(T - 1)
    for dx in range(1, X):
        send(r.vg.at[0], r.vx.at[dx - 1], (z * X + up_x(dx), n), vxi[dx - 1])

    ty.middle()
    for step in su.order():
        su.along_z(step)
    ty.finish()

    def close(i):
        rows = rows_of(i, 16)
        r.bo[rows, :] = (r.r1[rows, :] + ty.rows(rows) + r.vec[7:8, :]).astype(BF)

    loop(S // 16, close)
    sd.finish()

    def keep(i):
        rows = rows_of(i, 16)
        r.gd[rows, :] = sd.total(rows)

    loop(m.FD // 16, keep)
    for step in so.order():
        so.along_z(step)
    du, do, dq = Deal("u", su, r.gu), Deal("o", so, r.go), Deal("q", sq, r.gq)
    du.start()
    for step in sq.order():
        sq.along_z(step)
    total = r.vg[0]
    for dx in range(1, X):
        arrive(r.vx.at[dx - 1], vxi[dx - 1])
        total = total + r.vx[dx - 1]
    r.vg[1] = total
    for step in range(1, Z):
        send(r.vg.at[1], r.vz.at[step - 1], (up_z(step) * X + x, n), vzi[step - 1])
    do.start()
    dq.start()
    total = r.vg[1]
    for step in range(1, Z):
        arrive(r.vz.at[step - 1], vzi[step - 1])
        total = total + r.vz[step - 1]
    r.vg[2] = total
    for step in range(1, T):
        send(r.vg.at[2], r.vt.at[step - 1], (w, up_n(step)), vti[step - 1])
    du.finish()
    do.finish()
    dq.finish()
    total = r.vg[2]
    for step in range(1, T):
        arrive(r.vt.at[step - 1], vti[step - 1])
        total = total + r.vt[step - 1]
    r.gv[...] = total
    for one in sent:
        one.wait_send()


def block_step(m, args):
    scratch = scratch_of(m)
    kept = {"q": m.NQ, "o": m.Q, "u": m.F}
    grads = [
        jax.ShapeDtypeStruct((m.T, m.RD, cols) if m.inside else (m.RG, cols), BF)
        for cols in kept.values()
    ]
    vmem = pl.BlockSpec(memory_space=pltpu.VMEM)

    def kernel(*refs):
        block_kernel(m, list(scratch), *refs)

    return pl.pallas_call(
        kernel,
        out_shape=[
            jax.ShapeDtypeStruct((m.S, D), BF),
            jax.ShapeDtypeStruct((m.S, D), F32),
            *grads,
            jax.ShapeDtypeStruct((m.FD, D), F32),
            jax.ShapeDtypeStruct((16, D), F32),
        ],
        in_specs=[vmem] * len(args),
        out_specs=[vmem] * 7,
        scratch_shapes=[pltpu.VMEM(shape, kind) for shape, kind in scratch.values()]
        + [pltpu.SemaphoreType.DMA((semaphores_of(m),))],
        compiler_params=pltpu.CompilerParams(
            collective_id=0, has_side_effects=True, vmem_limit_bytes=62 * 1024 * 1024
        ),
        name="block_step",
    )(*args)


def body(
    tokens,
    cotangent,
    segment_ids,
    w_qkv,
    w_out,
    w_up,
    w_down,
    vectors,
    moments_qkv,
    moments_out,
    moments_up,
    moments_down,
    moments_vec,
):
    wide, narrow = lax.axis_size("wide"), lax.axis_size("narrow")
    m = layout(wide, narrow, tokens.shape[0])
    device = lax.axis_index("wide") * narrow + lax.axis_index("narrow")
    first_row = device * m.RD

    pq = w_qkv.astype(BF).reshape(m.RD, 3, m.T, m.Q).transpose(2, 0, 1, 3)
    po = w_out.astype(BF).reshape(m.RD, m.T, m.Q).transpose(1, 0, 2)
    pu = w_up.astype(BF).reshape(m.RD, m.W, m.T, m.FD).transpose(2, 0, 1, 3)
    parts = [pq.reshape(m.T, m.RD, m.NQ), po, pu.reshape(m.T, m.RD, m.F)]
    if not m.inside:
        parts = [
            lax.all_to_all(part, "narrow", 0, 0).reshape(m.RG, part.shape[2]) for part in parts
        ]
    low = vectors.astype(BF).T
    spot = jnp.zeros((12, D), BF)
    spot = lax.dynamic_update_slice(spot, low, (0, first_row))
    rise = spot[8:].reshape(m.W, m.T, m.FD).transpose(1, 0, 2).reshape(m.T, m.F)
    rise = jnp.pad(rise, ((0, 8 - m.T), (0, D - m.F)))
    packed = jnp.concatenate([spot[:8], rise], axis=0)
    segments = jnp.broadcast_to(segment_ids.astype(F32), (8, m.S))

    block_out, input_grad, gq, go, gu, gd, gv = block_step(
        m, (tokens, cotangent, segments, *parts, w_down.astype(BF), packed)
    )
    if not m.inside:
        gq, go, gu = [
            lax.all_to_all(g.reshape(m.T, m.RD, g.shape[1]), "narrow", 0, 0) for g in (gq, go, gu)
        ]
    grad_qkv = gq.reshape(m.T, m.RD, 3, m.Q).transpose(1, 2, 0, 3).reshape(m.RD, 3 * D)
    grad_out = go.transpose(1, 0, 2).reshape(m.RD, D)
    grad_up = gu.reshape(m.T, m.RD, m.W, m.FD).transpose(1, 2, 0, 3).reshape(m.RD, FF)
    rise = gv[8 : 8 + m.T, : m.F].reshape(m.T, m.W, m.FD).transpose(1, 0, 2).reshape(FF // D, D)
    grad_vec = lax.dynamic_slice(
        jnp.concatenate([gv[:8], rise], axis=0), (0, first_row), (12, m.RD)
    ).T

    new_qkv, state_qkv, copy_qkv = adam_update(
        w_qkv, moments_qkv, grad_qkv.astype(F32), RATE_MATRIX, WEIGHT_DECAY
    )
    new_out, state_out, copy_out = adam_update(
        w_out, moments_out, grad_out.astype(F32), RATE_MATRIX, WEIGHT_DECAY
    )
    new_up, state_up, copy_up = adam_update(
        w_up, moments_up, grad_up.astype(F32), RATE_MATRIX, WEIGHT_DECAY
    )
    new_down, state_down, copy_down = adam_update(w_down, moments_down, gd, RATE_MATRIX, WEIGHT_DECAY)
    new_vectors, state_vectors, copy_vectors = adam_update(
        vectors, moments_vec, grad_vec, RATE_VECTOR, 0.0
    )
    return (
        block_out,
        input_grad,
        new_qkv,
        new_out,
        new_up,
        new_down,
        new_vectors,
        state_qkv,
        state_out,
        state_up,
        state_down,
        state_vectors,
        copy_qkv,
        copy_out,
        copy_up,
        copy_down,
        copy_vectors,
    )


def solution(mesh):
    flat = P(("wide", "narrow"), None)
    pair = P(None, ("wide", "narrow"), None)
    return jax.shard_map(
        body,
        mesh=mesh,
        in_specs=(flat,) * 8 + (pair,) * 5,
        out_specs=(flat,) * 7 + (pair,) * 5 + (flat,) * 5,
        check_vma=False,
    )
```

time: 1130 us -> 256 us (0.23)
  waiting for transfers between devices: 965 us -> 0 us
  Pallas kernels: 0 us -> 225 us
  matrix products: 58.5 us -> 0 us
  blocking collectives: 43.8 us -> 0 us
  between operations: 14.4 us -> 0.94 us
    unnamed x12 -> x0, waiting for transfers between devices: 424 us -> none
    reduce_scatter x6 -> x0, waiting for transfers between devices: 312 us -> none  [the longest x1 68.8 us: body(): lax.psum_scatter(group_sums[3].astype(jnp.bfloat16), 'wide', scatter_dime...]
    all_gather x4 -> x0, waiting for transfers between devices: 228 us -> none  [the longest x1 77 us: body(): lax.all_gather(up_low, ('wide', 'narrow'), axis=0, tiled=True)]
    pallas_call x0 -> x1, Pallas kernels: none -> 225 us  [block_step(): pl.pallas_call(kernel, out_shape=[jax.ShapeDtypeStruct((m.S, D), BF), jax...]
    dot_general x18 -> x0, matrix products: 58.5 us -> none  [the longest x1 10.9 us: body(): jnp.einsum('sd,fd->sf', cotangent, down_back, preferred_element_type=jnp....]
    all_gather x1 -> x0, blocking collectives: 43.8 us -> none  [body(): lax.all_gather(vec_low, ('wide', 'narrow'), axis=0, tiled=True)]
  transfers between devices with their start and end apart: 11 -> 0, of which waited for: 11 -> 0; matrix products, arithmetic and copies ran while one was open for 5% -> 0% of each run, Pallas kernels for 0% -> 0%
where the time goes in v1:
time: 256 us; the launch traced here: 255 us
  Pallas kernels  225 us (88%)
  local copies, waits for them, and re-layouts  14.8 us (6%)
  other arithmetic  14.4 us (6%)
    pallas_call x1, Pallas kernels, block_step(): pl.pallas_call(kernel, out_shape=[jax.ShapeDtypeStruct((m.S, D), BF), jax...  225 us
    unnamed x47, local copies, waits for them, and re-layouts  8.58 us
    another operation x7, other arithmetic, adam_update(): jnp.stack([first_moment, second_moment])  6.11 us

profile of v1, /device:TPU:0, one launch (start us, length us, event | category | flops | bytes accessed | tf_op | source)
XLA Modules:
  0.0 255.0 jit_solution(5497351368245449134)
XLA Ops:
  0.7 0.0 copy-start.17
  0.7 0.7 copy-done.17
  1.4 0.1 dynamic_update_slice.3
  1.6 0.6 fusion.34.refs_7_
  2.2 1.1 convert_element_type.124
  3.3 0.2 reshape.169
  3.5 0.0 copy-start.4
  3.5 0.8 reshape.170.refs_5_
  4.3 0.2 copy-done.4
  4.5 0.1 reshape.166
  4.7 0.0 copy-start.2
  4.7 0.1 copy.101
  4.8 0.9 reshape.167.refs_3_
  5.7 0.0 copy-done.2
  5.7 0.7 convert_element_type.125.refs_6_
  6.4 0.2 copy-done.10
  6.6 0.6 copy.102
  7.3 0.0 copy-done.19
  7.3 0.6 broadcast_in_dim.11.refs_2_
  7.9 224.8 %block_step.1 = (bf16[128,1024]{1,0:T(8,128)(2,1)}, f32[128,1024]{1,0:T(8,128)}, bf16[4,32,768]{2,1,0:T(8,128)(2,1)}, bf16[4,32,256]{2,1,0:T(8,128)(2,1)}, bf16[...) custom-call(bf16[128,1024]{1,0:T(8,128)(2,1)} %refs_0_.1, bf16[128,1024]{1,0:T(8,128)(2,1)} %refs_1_.1, ...), custom_call_target="tpu_custom_call" | custom-call | tf_op jit(solution)/shard_map/block_step/pallas_call | solution.py:855
  232.7 0.0 copy-start.16
  232.7 0.8 slice_bitcast_fusion
  233.6 0.0 copy-done.16
  233.6 0.0 copy-start.18
  233.6 0.7 copy-done.18
  234.3 0.7 fusion.42
  235.0 0.6 copy.66
  235.7 0.0 copy-done.7
  235.7 2.3 fusion.21
  238.0 1.1 pad_maximum_fusion.1
  239.1 0.0 copy-done.12
  239.2 0.0 copy-start
  239.2 0.3 copy.59
  239.5 0.2 reshape.180
  239.7 0.6 copy-done
  240.4 0.1 multiply_add_fusion
  240.5 0.0 copy-start.14
  240.5 1.0 pad_maximum_fusion
  241.5 0.0 copy-done.14
  241.5 0.2 reshape.181
  241.8 0.0 copy-start.1
  241.8 0.3 copy.57
  242.0 0.2 reshape.178
  242.2 0.6 copy-done.1
  242.9 0.1 multiply_add_fusion.3
  243.0 0.0 copy-start.15
  243.0 0.9 pad_maximum_fusion.2
  243.9 0.0 copy-done.15
  243.9 0.7 convert_bitcast_fusion.1
  244.6 0.1 copy.58
  244.7 0.1 reshape.179
  244.8 0.8 copy-done.6
  245.6 0.7 pad_maximum_fusion.3
  246.3 1.0 reshape.177
  247.3 0.0 copy-done.3
  247.3 2.3 fusion.45
  249.7 0.2 reshape.175
  249.9 0.8 copy-done.5
  250.7 1.1 fusion.49
  251.8 0.0 copy-done.9
  251.8 0.9 copy-done.11
  252.7 0.8 fusion.47
  253.5 0.7 copy.109
  254.2 0.8 copy.110
  (35 shorter events, 0.3 us)
Async XLA Ops:
  0.7 0.7 copy-start.17
  3.5 1.0 copy-start.4
  4.7 1.0 copy-start.2
  5.7 0.9 copy-start.10
  5.7 1.6 copy-start.19
  6.6 229.0 %copy-start.7 = (f32[2,128,1024]{2,1,0:T(8,128)S(1)}, f32[2,128,1024]{2,1,0:T(8,128)}, u32[]{:S(2)}) copy-start(f32[2,128,1024]{2,1,0:T(8,128)} %param.24) | copy-start | bytes 3145732
  232.7 0.9 copy-start.16
  233.6 0.7 copy-start.18
  238.0 1.1 copy-start.12
  239.2 1.2 copy-start
  240.5 1.1 copy-start.14
  241.8 1.1 copy-start.1
  243.0 0.9 copy-start.15
  244.6 0.9 copy-start.6
  246.3 1.0 copy-start.3
  249.7 1.0 copy-start.5
  250.7 1.1 copy-start.9
  251.8 0.9 copy-start.11
  251.8 1.7 copy-start.13
  252.7 1.5 copy-start.8

commit v2 on v1

--- a/solution.py
+++ b/solution.py
@@ -47,12 +47,12 @@
     return lax.dot_general(left, right, (((0,), (0,)), ((), ())), preferred_element_type=F32)
 
 
-def loop(count, body):
+def loop(count, body, first=0):
     def step(index, carry):
         body(index)
         return carry
 
-    lax.fori_loop(0, count, step, 0)
+    lax.fori_loop(first, first + count, step, 0)
 
 
 def normalize(rows):
@@ -240,21 +240,23 @@
             self.xi = fresh(Z * (X - 1))
 
         def along_z(self):
-            for step in range(1, Z):
-                send(self.ref.at[w], self.ref.at[w], (up_z(step) * X + x, n), self.zi[step - 1])
+            for k in range(Z - 1):
+                step = 1 + lax.rem(k + 1 - lax.rem(z, 2), Z - 1)
+                send(self.ref.at[w], self.ref.at[w], (up_z(step) * X + x, n), self.zi[0] + step - 1)
 
         def forward(self, step):
-            block = down_z(step) * X + x if step else w
+            block = down_z(step) * X + x
             for dx in range(1, X):
                 send(
                     self.ref.at[block],
                     self.ref.at[block],
                     (z * X + up_x(dx), n),
-                    self.xi[step * (X - 1) + dx - 1],
+                    self.xi[0] + step * (X - 1) + dx - 1,
                 )
 
-        def relay(self, step):
-            arrive(self.ref.at[down_z(step) * X + x], self.zi[step - 1])
+        def relay(self, k):
+            step = jnp.where(lax.rem(z, 2) == 0, k, Z - k)
+            arrive(self.ref.at[down_z(step) * X + x], self.zi[0] + step - 1)
             self.forward(step)
 
         def relays(self):
@@ -284,8 +286,7 @@
                 arrive(self.slot(block), self.yi[step - 1])
                 send(self.slot(block), self.slot(block), sibling, self.ci[step])
 
-        def finish(self):
-            self.middle()
+        def close(self):
             for step in range(Y):
                 block = 2 * at_y(-step) + 1 - c
                 arrive(self.slot(block), self.ci[step])
@@ -347,7 +348,7 @@
                 self.chunk = 16
 
         def order(self):
-            return list(range(1, Z)) + [0]
+            return [Z // 2] + [k for k in range(1, Z) if k != Z // 2] + [0]
 
         def multiply(self, step, left, right):
             first = up_z(step) if step else z
@@ -461,34 +462,48 @@
     so, sq = Scatter("o", m.RG, m.Q), Scatter("q", m.RG, m.NQ)
 
     vi, si = fresh(T - 1), fresh(T - 1)
+    for step in range(1, T):
+        send(r.pv, r.vn.at[step - 1], (w, up_n(step)), vi[step - 1])
+    r.wd[w] = r.pd[...]
+    gd.forward(0)
+
+    class Rows:
+        def __init__(self, part, target):
+            self.part, self.target = part, target
+            self.ids = fresh(T - 1) if m.inside else []
+
+        def at(self, k, rows):
+            return r.wo.at[k, w, rows] if self.target is None else self.target.at[w, rows]
+
+        def start(self):
+            if m.inside:
+                own = pl.ds(pl.multiple_of(n * m.RD, m.RD), m.RD)
+                for step in range(1, T):
+                    other = up_n(step)
+                    send(self.part.at[other], self.at(other, own), (w, other), self.ids[step - 1])
+                self.at(n, own)[...] = self.part[n]
+            elif self.target is None:
+                r.wo[n, w] = self.part[...]
+            else:
+                self.target[w] = self.part[...]
+
+        def finish(self):
+            if m.inside:
+                for step in range(1, T):
+                    got = pl.ds(pl.multiple_of(down_n(step) * m.RD, m.RD), m.RD)
+                    arrive(self.at(n, got), self.ids[step - 1])
+
+    ro, rq, ru = Rows(r.po, None), Rows(r.pq, r.wq), Rows(r.pu, r.wu)
+    ro.start()
+    rq.start()
+    own_rows = rows_of(n, S)
+    r.tok[own_rows, :] = r.x[...]
+    tokens.start()
     r.sg[n] = r.seg[...]
     for step in range(1, T):
-        send(r.pv, r.vn.at[step - 1], (w, up_n(step)), vi[step - 1])
-    shares = []
-    if m.inside:
-        for part, target in ((r.po, None), (r.pq, r.wq), (r.pu, r.wu)):
-            ids = fresh(T - 1)
-            own = pl.ds(pl.multiple_of(n * m.RD, m.RD), m.RD)
-            for step in range(1, T):
-                other = up_n(step)
-                there = r.wo.at[other, w, own] if target is None else target.at[w, own]
-                send(part.at[other], there, (w, other), ids[step - 1])
-            shares.append((target, ids))
-            if target is None:
-                r.wo[n, w, own, :] = part[n]
-            else:
-                target[w, own, :] = part[n]
-    else:
-        r.wo[n, w] = r.po[...]
-        r.wq[w] = r.pq[...]
-        r.wu[w] = r.pu[...]
-    r.wd[w] = r.pd[...]
-    own_rows = rows_of(n, S)
-    r.tok[own_rows, :] = r.x[...]
+        send(r.sg.at[n], r.sg.at[n], (w, up_n(step)), si[step - 1])
+    ru.start()
     r.dya[own_rows, :] = r.dy[...]
-    for step in range(1, T):
-        send(r.sg.at[n], r.sg.at[n], (w, up_n(step)), si[step - 1])
-    tokens.start()
     cotangents.start()
 
     vector = r.pv[...].astype(F32)
@@ -498,26 +513,19 @@
     r.wv[w] = vector.astype(BF)
     gv.along_z()
     gv.forward(0)
-
-    def shared(k):
-        if m.inside:
-            target, ids = shares[k]
-            for step in range(1, T):
-                got = pl.ds(pl.multiple_of(down_n(step) * m.RD, m.RD), m.RD)
-                arrive(r.wo.at[n, w, got] if target is None else target.at[w, got], ids[step - 1])
-
-    shared(0)
+    ro.finish()
     go.along_z()
     go.forward(0)
-    shared(1)
+    rq.finish()
     gq.along_z()
-    shared(2)
+    gv.relays()
+    tokens.middle()
+    ru.finish()
     gu.along_z()
     gd.along_z()
-    gv.relays()
     go.relays()
     gq.forward(0)
-    tokens.finish()
+    tokens.close()
     gv.finish()
     vector = r.wv[0].astype(F32)
     for k in range(1, m.W):
@@ -534,14 +542,19 @@
         unit, _ = normalize(r.tok[rows, :].astype(F32))
         r.a[rows, :] = (unit * r.vec[0:1, :] + r.vec[1:2, :]).astype(BF)
 
-    loop(L // 16, first_norm)
-    cotangents.finish()
+    half = L // 32
+    loop(half, first_norm)
+    cotangents.middle()
     go.finish()
     outs.start()
+    gq.relay(1)
+    loop(half, first_norm, half)
+    for k in range(2, Z - 1):
+        gq.relay(k)
     transpose(r.at, lambda i, j: r.a[i, j], L // 128, D // 128)
-    gq.relays()
+    gq.relay(Z - 1)
     gu.forward(0)
-    outs.middle()
+    cotangents.close()
     gq.finish()
 
     tile_q = 256 if m.NQ % 256 == 0 else 128
@@ -554,6 +567,8 @@
     loop(m.NQ // tile_q, project)
     for step in range(1, T):
         arrive(r.sg.at[down_n(step)], si[step - 1])
+    gu.relay(1)
+    outs.middle()
 
     lane = lax.broadcasted_iota(jnp.int32, (1, 128), 1)
     halves = [(lane // HEAD == k).astype(F32) for k in range(128 // HEAD)]
@@ -586,14 +601,12 @@
 
     loop(T, attend)
     mixes.start()
-    gu.relay(1)
     for k in range(2, Z - 1):
         gu.relay(k)
+    outs.close()
     mixes.middle()
-    for step in range(Y):
-        arrive(outs.slot(2 * at_y(-step) + 1 - c), outs.ci[step])
-    for step in range(Y):
-        arrive(mixes.slot(2 * at_y(-step) + 1 - c), mixes.ci[step])
+    gu.relay(Z - 1)
+    mixes.close()
 
     for t in range(T):
         r.oo[:, t * m.Q : (t + 1) * m.Q] = r.oa[t, own_rows, :]
@@ -610,8 +623,8 @@
 
     loop(S // 16, second_norm)
     seconds.start()
-    gu.relay(Z - 1)
-    gd.forward(0)
+    for k in range(1, Z - 1):
+        gd.relay(k)
     seconds.middle()
     for t in range(T):
         for k in range(m.Q // 128):
@@ -622,8 +635,8 @@
                 r.ot[base : base + 128, rows_of(i, 128)] = value.T.astype(BF)
 
             loop(L // 128, turn)
-    for step in range(Y):
-        arrive(seconds.slot(2 * at_y(-step) + 1 - c), seconds.ci[step])
+    seconds.close()
+    gd.relay(Z - 1)
     transpose(r.ct, lambda i, j: r.ca[i, j], L // 128, D // 128)
     gu.finish()
 
@@ -643,11 +656,12 @@
 
     loop(L // 16, activate)
     transpose(r.ht, lambda i, j: r.h[i, j], L // 128, m.F // 128)
-    for step in sd.order():
+    sd.multiply(sd.order()[0], r.ht, r.dya)
+    sd.along_x(sd.order()[0])
+    for step in sd.order()[1:]:
         sd.multiply(step, r.ht, r.dya)
-    gd.relays()
-    for step in sd.order():
         sd.along_x(step)
+    sd.along_z(sd.order()[0])
     gd.finish()
 
     group = 256 // m.FD
@@ -678,7 +692,8 @@
         r.Py[:, cols] = nn(r.h[...], r.wd[:, :, cols].reshape(m.F, 256)).astype(BF)
 
     loop(D // 256, contract)
-    sd.along_z(1)
+    ty.start()
+    sd.along_z(sd.order()[1])
     tc.finish()
     r.sums[0:4] = jnp.zeros((4, 16, D), F32)
 
@@ -714,8 +729,8 @@
         r.dab[step] = r.da[:, rows_of(other, m.Q)]
         send(r.dab.at[step], r.daq.at[own_rows], (w, other), ai[step - 1])
     r.daq[own_rows, :] = r.da[:, rows_of(n, m.Q)]
-    ty.start()
-    sd.along_z(2 if Z > 2 else 0)
+    for step in sd.order()[2:-1]:
+        sd.along_z(step)
     for step in range(1, T):
         arrive(r.dof.at[rows_of(down_n(step), S)], oi[step - 1])
 
@@ -738,7 +753,11 @@
             r.dqkv[rows, at[1]] = (pick(dk) * scale).astype(BF)
             r.dqkv[rows, at[2]] = pick(dv).astype(BF)
 
-    loop(T, attend_back)
+    loop(T // 2, attend_back)
+    su.along_z(su.order()[0])
+    loop(T - T // 2, attend_back, T // 2)
+    sd.along_z(sd.order()[-1])
+    ty.middle()
 
     def project_back(j):
         value = nt(r.dqkv[...], r.wq[rows_of(j, width)].reshape(256, m.NQ))
@@ -752,11 +771,11 @@
         so.multiply(step, r.ot, r.daq)
         so.along_x(step)
     tin.middle()
+    su.along_z(su.order()[1])
     for step in sq.order():
         sq.multiply(step, r.at, r.dqkv)
-        sq.along_x(step)
-    for step in sd.order()[2:]:
-        sd.along_z(step)
+    for step in su.order()[2:-1]:
+        su.along_z(step)
 
     r.vg[0] = jnp.zeros((16, D), F32)
     for k, row in enumerate((4, 5, 6, 7)):
@@ -789,9 +808,9 @@
     for dx in range(1, X):
         send(r.vg.at[0], r.vx.at[dx - 1], (z * X + up_x(dx), n), vxi[dx - 1])
 
-    ty.middle()
-    for step in su.order():
-        su.along_z(step)
+    for step in sq.order():
+        sq.along_x(step)
+    su.along_z(su.order()[-1])
     ty.finish()
 
     def close(i):
@@ -799,19 +818,8 @@
         r.bo[rows, :] = (r.r1[rows, :] + ty.rows(rows) + r.vec[7:8, :]).astype(BF)
 
     loop(S // 16, close)
-    sd.finish()
-
-    def keep(i):
-        rows = rows_of(i, 16)
-        r.gd[rows, :] = sd.total(rows)
-
-    loop(m.FD // 16, keep)
     for step in so.order():
         so.along_z(step)
-    du, do, dq = Deal("u", su, r.gu), Deal("o", so, r.go), Deal("q", sq, r.gq)
-    du.start()
-    for step in sq.order():
-        sq.along_z(step)
     total = r.vg[0]
     for dx in range(1, X):
         arrive(r.vx.at[dx - 1], vxi[dx - 1])
@@ -819,6 +827,19 @@
     r.vg[1] = total
     for step in range(1, Z):
         send(r.vg.at[1], r.vz.at[step - 1], (up_z(step) * X + x, n), vzi[step - 1])
+    sd.finish()
+
+    def keep(i):
+        rows = rows_of(i, 16)
+        r.gd[rows, :] = sd.total(rows)
+
+    loop(m.FD // 16, keep)
+    du, do, dq = Deal("u", su, r.gu), Deal("o", so, r.go), Deal("q", sq, r.gq)
+    for step in sq.order()[:2]:
+        sq.along_z(step)
+    du.start()
+    for step in sq.order()[2:]:
+        sq.along_z(step)
     do.start()
     dq.start()
     total = r.vg[1]

time: 256 us -> 230 us (0.90)
  Pallas kernels: 225 us -> 199 us
    pallas_call x1, Pallas kernels: 225 us -> 199 us  [block_step(): pl.pallas_call(kernel, out_shape=[jax.ShapeDtypeStruct((m.S, D), BF), jax...]
where the time goes in v2:
time: 230 us; the launch traced here: 229 us
  Pallas kernels  199 us (87%)
  local copies, waits for them, and re-layouts  14.8 us (6%)
  other arithmetic  14.4 us (6%)
    pallas_call x1, Pallas kernels, block_step(): pl.pallas_call(kernel, out_shape=[jax.ShapeDtypeStruct((m.S, D), BF), jax...  199 us
    unnamed x47, local copies, waits for them, and re-layouts  8.58 us
    another operation x7, other arithmetic, adam_update(): jnp.stack([first_moment, second_moment])  6.11 us
    convert_element_type x4, other arithmetic, adam_update(): updated.astype(BF)  4.9 us

profile of v2, /device:TPU:0, one launch (start us, length us, event | category | flops | bytes accessed | tf_op | source)
XLA Modules:
  0.0 228.8 jit_solution(13700982721258805136)
XLA Ops:
  0.7 0.0 copy-start.17
  0.7 0.7 copy-done.17
  1.4 0.1 dynamic_update_slice.3
  1.6 0.6 fusion.34.refs_7_
  2.2 1.1 convert_element_type.124
  3.3 0.2 reshape.169
  3.5 0.0 copy-start.4
  3.5 0.8 reshape.170.refs_5_
  4.3 0.2 copy-done.4
  4.5 0.1 reshape.166
  4.7 0.0 copy-start.2
  4.7 0.1 copy.101
  4.8 0.9 reshape.167.refs_3_
  5.7 0.0 copy-done.2
  5.7 0.7 convert_element_type.125.refs_6_
  6.4 0.2 copy-done.10
  6.6 0.6 copy.102
  7.3 0.0 copy-done.19
  7.3 0.6 broadcast_in_dim.11.refs_2_
  7.9 198.7 %block_step.1 = (bf16[128,1024]{1,0:T(8,128)(2,1)}, f32[128,1024]{1,0:T(8,128)}, bf16[4,32,768]{2,1,0:T(8,128)(2,1)}, bf16[4,32,256]{2,1,0:T(8,128)(2,1)}, bf16[...) custom-call(bf16[128,1024]{1,0:T(8,128)(2,1)} %refs_0_.1, bf16[128,1024]{1,0:T(8,128)(2,1)} %refs_1_.1, ...), custom_call_target="tpu_custom_call" | custom-call | tf_op jit(solution)/shard_map/block_step/pallas_call | solution.py:876
  206.6 0.0 copy-start.16
  206.6 0.8 slice_bitcast_fusion
  207.5 0.0 copy-done.16
  207.5 0.0 copy-start.18
  207.5 0.7 copy-done.18
  208.2 0.7 fusion.42
  208.9 0.6 copy.66
  209.5 0.0 copy-done.7
  209.5 2.3 %fusion.21 = (f32[1,128,1024]{2,1,0:T(8,128)S(1)}, f32[1,128,1024]{2,1,0:T(8,128)S(1)}, bf16[128,1024]{1,0:T(8,128)(2,1)}, f32[128,1024]{1,0:T(8,128)}) fusion(f32[128,1024]{1,0:T(8,128)} %get-tuple-element.29, f32[2,128,1024]{2,1,0:T(8,128)S(1)} %copy-done.7, f32[128,1024]{1,0:T(8,128)S(1)} %copy-done.2), kind=kLoop, calls=%fused_computation.49 | loop fusion | flops 1966080 | bytes 3932160 | tf_op jit(solution)/shard_map/stack | solution.py:35
  211.8 1.1 pad_maximum_fusion.1
  212.9 0.0 copy-done.12
  213.0 0.0 copy-start
  213.0 0.3 copy.59
  213.4 0.2 reshape.180
  213.6 0.6 copy-done
  214.3 0.1 multiply_add_fusion
  214.4 0.0 copy-start.14
  214.4 1.0 pad_maximum_fusion
  215.4 0.0 copy-done.14
  215.4 0.2 reshape.181
  215.6 0.0 copy-start.1
  215.6 0.3 copy.57
  215.9 0.2 reshape.178
  216.1 0.6 copy-done.1
  216.8 0.1 multiply_add_fusion.3
  216.9 0.0 copy-start.15
  216.9 0.9 pad_maximum_fusion.2
  217.8 0.0 copy-done.15
  217.8 0.7 convert_bitcast_fusion.1
  218.5 0.1 copy.58
  218.6 0.1 reshape.179
  218.6 0.8 copy-done.6
  219.5 0.7 pad_maximum_fusion.3
  220.2 1.0 reshape.177
  221.2 0.0 copy-done.3
  221.2 2.3 %fusion.45 = (bf16[32,4096]{1,0:T(8,128)(2,1)}, f32[32,4096]{1,0:T(8,128)}) fusion(f32[32,4096]{1,0:T(8,128)S(1)} %copy-done.3, f32[32,4096]{1,0:T(8,128)} %reshape.177, f32[2,32,4096]{2,1,0:T(8,128)S(1)} %copy-done), kind=kLoop, calls=%fused_computation.90 | loop fusion | flops 1966080 | bytes 2883584 | tf_op jit(solution)/shard_map/convert_element_type | solution.py:35
  223.5 0.2 reshape.175
  223.7 0.8 copy-done.5
  224.5 1.1 fusion.49
  225.6 0.0 copy-done.9
  225.7 0.9 copy-done.11
  226.5 0.8 fusion.47
  227.3 0.7 copy.109
  228.0 0.8 copy.110
  (35 shorter events, 0.3 us)
Async XLA Ops:
  0.7 0.7 copy-start.17
  3.5 1.0 copy-start.4
  4.7 1.0 copy-start.2
  5.7 0.9 copy-start.10
  5.7 1.6 copy-start.19
  6.6 202.9 %copy-start.7 = (f32[2,128,1024]{2,1,0:T(8,128)S(1)}, f32[2,128,1024]{2,1,0:T(8,128)}, u32[]{:S(2)}) copy-start(f32[2,128,1024]{2,1,0:T(8,128)} %param.24) | copy-start | bytes 3145732
  206.6 0.9 copy-start.16
  207.5 0.7 copy-start.18
  211.8 1.1 copy-start.12
  213.0 1.2 copy-start
  214.4 1.1 copy-start.14
  215.6 1.1 copy-start.1
  216.9 0.9 copy-start.15
  218.5 0.9 copy-start.6
  220.2 1.0 copy-start.3
  223.5 1.0 copy-start.5
  224.5 1.1 copy-start.9
  225.6 0.9 copy-start.11
  225.6 1.7 copy-start.13
  226.5 1.5 copy-start.8

commit v3 on v2

--- a/solution.py
+++ b/solution.py
@@ -83,6 +83,7 @@
     m.FD = FF // (wide * narrow)
     m.NH = m.Q // HEAD
     m.inside = m.RD % 16 == 0
+    m.line = m.Z == 4
     return m
 
 
@@ -97,7 +98,7 @@
             "G" + name: ((m.W, rows, cols), BF),
             "X" + name: ((m.X - 1, m.Z, rows, cols), BF),
             "S" + name: ((m.Z, rows, cols), BF),
-            "Z" + name: ((m.Z - 1, rows, cols), BF),
+            "Z" + name: ((m.Z if m.line else m.Z - 1, rows, cols), BF),
         }
 
     def spread(name, cols):
@@ -166,8 +167,8 @@
 
 
 def semaphores_of(m):
-    gather = (m.Z - 1) + m.Z * (m.X - 1)
-    scatter = m.Z * (m.X - 1) + (m.Z - 1)
+    gather = 2 * m.Z + m.Z * (m.X - 1)
+    scatter = m.Z * (m.X - 1) + 2 * m.Z
     pair = (m.Y - 1) + m.Y
     direct = m.T - 1
     total = 5 * gather + 4 * scatter + 8 * pair + 10 * direct + (m.X - 1) + (m.Z - 1) + direct
@@ -191,20 +192,27 @@
         used[0] += count
         return [first + k for k in range(count)]
 
-    def copy(src, dst, device, index):
+    inner = (z == 1) | (z == 2)
+    mate = jnp.where(z < 2, 1 - z, 5 - z)
+    fin, fend = jnp.where(z < 2, 2, 1), jnp.where(z < 2, 3, 0)
+
+    def copy(src, dst, device, index, out=None):
         return pltpu.make_async_remote_copy(
             src_ref=src,
             dst_ref=dst,
-            send_sem=r.sem.at[2 * index],
+            send_sem=r.sem.at[2 * (index if out is None else out)],
             recv_sem=r.sem.at[2 * index + 1],
             device_id=device,
             device_id_type=MESH,
         )
 
-    def send(src, dst, device, index):
-        one = copy(src, dst, device, index)
-        one.start()
-        sent.append(one)
+    def send(src, dst, device, index, out=None, only=None):
+        one = copy(src, dst, device, index, out)
+        if only is None:
+            one.start()
+        else:
+            pl.when(only)(one.start)
+        sent.append((one, only))
 
     def arrive(dst, index):
         copy(dst, dst, sibling, index).wait_recv()
@@ -236,38 +244,65 @@
     class Gather:
         def __init__(self, ref):
             self.ref = ref
-            self.zi = fresh(Z - 1)
-            self.xi = fresh(Z * (X - 1))
+            self.zi = fresh(Z - 1)[0]
+            self.out = fresh(4)
+            self.xi = fresh(Z * (X - 1))[0]
+
+        def to_z(self, block, there, index, out, only=None):
+            send(self.ref.at[block], self.ref.at[block], (there * X + x, n), self.zi + index, out, only)
 
         def along_z(self):
-            for k in range(Z - 1):
-                step = 1 + lax.rem(k + 1 - lax.rem(z, 2), Z - 1)
-                send(self.ref.at[w], self.ref.at[w], (up_z(step) * X + x, n), self.zi[0] + step - 1)
-
-        def forward(self, step):
+            if m.line:
+                self.to_z(w, fin, jnp.where(inner, 1, 2), self.out[0])
+                self.to_z(w, mate, 0, self.out[1])
+                return
+            for step in range(1, Z):
+                self.to_z(w, up_z(step), step - 1, None)
+
+        def forward(self, step, only=None):
             block = down_z(step) * X + x
             for dx in range(1, X):
                 send(
                     self.ref.at[block],
                     self.ref.at[block],
                     (z * X + up_x(dx), n),
-                    self.xi[0] + step * (X - 1) + dx - 1,
+                    self.xi + step * (X - 1) + dx - 1,
+                    only=only,
                 )
 
-        def relay(self, k):
-            step = jnp.where(lax.rem(z, 2) == 0, k, Z - k)
-            arrive(self.ref.at[down_z(step) * X + x], self.zi[0] + step - 1)
-            self.forward(step)
-
-        def relays(self):
-            for step in range(1, Z):
-                self.relay(step)
+        def relay(self, k, who):
+            if not m.line and who == "end":
+                return
+            only = None
+            if m.line:
+                only = inner if who == "inner" else jnp.logical_not(inner)
+            step, index = k, k - 1
+            if m.line:
+                index = jnp.where(inner, k % 3, k - 1)
+                there = jnp.where(index == 0, mate, jnp.where(index == 1, fin, fend))
+                step = lax.rem(z + Z - there, Z)
+            block = down_z(step) * X + x
+            if only is None:
+                arrive(self.ref.at[block], self.zi + index)
+            else:
+                pl.when(only)(lambda: arrive(self.ref.at[block], self.zi + index))
+            if m.line and k < 3 and who == "inner":
+                self.to_z(block, mate, index, self.out[1 + k], inner)
+            self.forward(step, only)
+
+        def inside(self, steps):
+            for k in steps:
+                self.relay(k, "inner")
+
+        def ends(self, steps):
+            for k in steps:
+                self.relay(k, "end")
 
         def finish(self):
             for step in range(Z):
                 for dx in range(1, X):
                     block = (down_z(step) if step else z) * X + down_x(dx)
-                    arrive(self.ref.at[block], self.xi[step * (X - 1) + dx - 1])
+                    arrive(self.ref.at[block], self.xi + step * (X - 1) + dx - 1)
 
     class Share:
         def __init__(self, slot):
@@ -342,16 +377,22 @@
             self.sums = getattr(r, "S" + name)
             self.fromz = getattr(r, "Z" + name)
             self.xi = fresh(Z * (X - 1))
-            self.zi = fresh(Z - 1)
+            self.zi = fresh(Z)[0]
+            self.out = fresh(Z - 1)
             self.chunk = 16 if cols > 512 else 32
             if rows % self.chunk:
                 self.chunk = 16
 
         def order(self):
-            return [Z // 2] + [k for k in range(1, Z) if k != Z // 2] + [0]
-
-        def multiply(self, step, left, right):
-            first = up_z(step) if step else z
+            return list(range(Z))
+
+        def there(self, k):
+            if k == Z - 1:
+                return z
+            return (fin, fend, mate)[k] if m.line else up_z(k + 1)
+
+        def multiply(self, k, left, right):
+            first = self.there(k)
             high = X * self.rows
             tile = 256 if self.cols % 256 == 0 else 128
 
@@ -363,41 +404,80 @@
 
             loop(self.cols // tile, one)
 
-        def along_x(self, step):
-            first = up_z(step) if step else z
+        def along_x(self, k):
+            first = self.there(k)
             for dx in range(1, X):
                 other = up_x(dx)
                 send(
                     self.grad.at[first * X + other],
-                    self.fromx.at[dx - 1, step],
+                    self.fromx.at[dx - 1, k],
                     (z * X + other, n),
-                    self.xi[step * (X - 1) + dx - 1],
+                    self.xi[k * (X - 1) + dx - 1],
                 )
 
-        def along_z(self, step):
-            block = (up_z(step) if step else z) * X + x
+        def along_z(self, k):
+            block = self.there(k) * X + x
             for dx in range(1, X):
-                arrive(self.fromx.at[dx - 1, step], self.xi[step * (X - 1) + dx - 1])
+                arrive(self.fromx.at[dx - 1, k], self.xi[k * (X - 1) + dx - 1])
 
             def add(i):
                 rows = rows_of(i, self.chunk)
                 total = self.grad[block, rows, :].astype(F32)
                 for dx in range(1, X):
-                    total = total + self.fromx[dx - 1, step, rows, :].astype(F32)
-                self.sums[step, rows, :] = total.astype(BF)
+                    total = total + self.fromx[dx - 1, k, rows, :].astype(F32)
+                self.sums[k, rows, :] = total.astype(BF)
 
             loop(self.rows // self.chunk, add)
-            if step:
-                send(self.sums.at[step], self.fromz.at[step - 1], (block, n), self.zi[step - 1])
+            if k == Z - 1:
+                return
+            if not m.line:
+                self.to_z(k, block, k)
+            elif k == 2:
+                self.to_z(k, mate * X + x, 2)
+            else:
+                self.to_z(k, mate * X + x, k, z != jnp.where(z < 2, 1, 2))
+
+        def to_z(self, k, block, slot, only=None):
+            send(self.sums.at[k], self.fromz.at[slot], (block, n), self.zi + slot, self.out[k], only)
+
+        def join(self, k):
+            if not m.line:
+                return
+
+            @pl.when(inner)
+            def _():
+                arrive(self.fromz.at[k], self.zi + k)
+
+                def add(i):
+                    rows = rows_of(i, self.chunk)
+                    total = self.sums[k, rows, :].astype(F32) + self.fromz[k, rows, :].astype(F32)
+                    self.sums[k, rows, :] = total.astype(BF)
+
+                loop(self.rows // self.chunk, add)
+                copy(
+                    self.sums.at[k], self.fromz.at[3], (self.there(k) * X + x, n), self.zi + 3, self.out[k]
+                ).start()
+
+            sent.append(
+                (
+                    copy(
+                        self.sums.at[k], self.fromz.at[3], (self.there(k) * X + x, n), self.zi + 3, self.out[k]
+                    ),
+                    inner,
+                )
+            )
+
+        def last(self):
+            return [2, 3] if m.line else list(range(Z - 1))
 
         def finish(self):
-            for step in range(1, Z):
-                arrive(self.fromz.at[step - 1], self.zi[step - 1])
+            for slot in self.last():
+                arrive(self.fromz.at[slot], self.zi + slot)
 
         def total(self, rows):
-            total = self.sums[0, rows, :].astype(F32)
-            for step in range(1, Z):
-                total = total + self.fromz[step - 1, rows, :].astype(F32)
+            total = self.sums[Z - 1, rows, :].astype(F32)
+            for slot in self.last():
+                total = total + self.fromz[slot, rows, :].astype(F32)
             return total
 
     class Deal:
@@ -511,20 +591,21 @@
         arrive(r.vn.at[step - 1], vi[step - 1])
         vector = vector + r.vn[step - 1].astype(F32)
     r.wv[w] = vector.astype(BF)
+    early, late = range(1, Z - 1), range(Z - 1, Z)
     gv.along_z()
     gv.forward(0)
     ro.finish()
     go.along_z()
     go.forward(0)
+    gv.inside(early)
     rq.finish()
     gq.along_z()
-    gv.relays()
+    gq.forward(0)
+    go.inside(early)
     tokens.middle()
     ru.finish()
-    gu.along_z()
-    gd.along_z()
-    go.relays()
-    gq.forward(0)
+    gv.inside(late)
+    gv.ends(range(1, Z))
     tokens.close()
     gv.finish()
     vector = r.wv[0].astype(F32)
@@ -543,16 +624,20 @@
         r.a[rows, :] = (unit * r.vec[0:1, :] + r.vec[1:2, :]).astype(BF)
 
     half = L // 32
+    gq.inside(early)
+    gu.along_z()
+    go.inside(late)
+    go.ends(range(1, Z))
     loop(half, first_norm)
     cotangents.middle()
+    gq.inside(late)
+    gq.ends(range(1, 2))
     go.finish()
     outs.start()
-    gq.relay(1)
     loop(half, first_norm, half)
-    for k in range(2, Z - 1):
-        gq.relay(k)
+    gq.ends(range(2, Z - 1))
     transpose(r.at, lambda i, j: r.a[i, j], L // 128, D // 128)
-    gq.relay(Z - 1)
+    gq.ends(late)
     gu.forward(0)
     cotangents.close()
     gq.finish()
@@ -567,7 +652,9 @@
     loop(m.NQ // tile_q, project)
     for step in range(1, T):
         arrive(r.sg.at[down_n(step)], si[step - 1])
-    gu.relay(1)
+    gu.inside(early)
+    gd.along_z()
+    gu.ends(range(1, 2))
     outs.middle()
 
     lane = lax.broadcasted_iota(jnp.int32, (1, 128), 1)
@@ -601,11 +688,11 @@
 
     loop(T, attend)
     mixes.start()
-    for k in range(2, Z - 1):
-        gu.relay(k)
+    gu.inside(late)
+    gu.ends(range(2, Z - 1))
     outs.close()
     mixes.middle()
-    gu.relay(Z - 1)
+    gu.ends(late)
     mixes.close()
 
     for t in range(T):
@@ -623,8 +710,8 @@
 
     loop(S // 16, second_norm)
     seconds.start()
-    for k in range(1, Z - 1):
-        gd.relay(k)
+    gd.inside(early)
+    gd.ends(range(1, 2))
     seconds.middle()
     for t in range(T):
         for k in range(m.Q // 128):
@@ -636,8 +723,10 @@
 
             loop(L // 128, turn)
     seconds.close()
-    gd.relay(Z - 1)
+    gd.inside(late)
+    gd.ends(range(2, Z - 1))
     transpose(r.ct, lambda i, j: r.ca[i, j], L // 128, D // 128)
+    gd.ends(late)
     gu.finish()
 
     def expand(j):
@@ -693,7 +782,7 @@
 
     loop(D // 256, contract)
     ty.start()
-    sd.along_z(sd.order()[1])
+    sd.along_z(1)
     tc.finish()
     r.sums[0:4] = jnp.zeros((4, 16, D), F32)
 
@@ -731,6 +820,7 @@
     r.daq[own_rows, :] = r.da[:, rows_of(n, m.Q)]
     for step in sd.order()[2:-1]:
         sd.along_z(step)
+    sd.join(0)
     for step in range(1, T):
         arrive(r.dof.at[rows_of(down_n(step), S)], oi[step - 1])
 
@@ -757,6 +847,7 @@
     su.along_z(su.order()[0])
     loop(T - T // 2, attend_back, T // 2)
     sd.along_z(sd.order()[-1])
+    sd.join(1)
     ty.middle()
 
     def project_back(j):
@@ -771,11 +862,12 @@
         so.multiply(step, r.ot, r.daq)
         so.along_x(step)
     tin.middle()
-    su.along_z(su.order()[1])
+    su.along_z(1)
     for step in sq.order():
         sq.multiply(step, r.at, r.dqkv)
     for step in su.order()[2:-1]:
         su.along_z(step)
+    su.join(0)
 
     r.vg[0] = jnp.zeros((16, D), F32)
     for k, row in enumerate((4, 5, 6, 7)):
@@ -810,6 +902,7 @@
 
     for step in sq.order():
         sq.along_x(step)
+    su.join(1)
     su.along_z(su.order()[-1])
     ty.finish()
 
@@ -820,6 +913,8 @@
     loop(S // 16, close)
     for step in so.order():
         so.along_z(step)
+    so.join(0)
+    so.join(1)
     total = r.vg[0]
     for dx in range(1, X):
         arrive(r.vx.at[dx - 1], vxi[dx - 1])
@@ -837,9 +932,12 @@
     du, do, dq = Deal("u", su, r.gu), Deal("o", so, r.go), Deal("q", sq, r.gq)
     for step in sq.order()[:2]:
         sq.along_z(step)
+    sq.join(0)
+    for step in sq.order()[2:-1]:
+        sq.along_z(step)
+    sq.join(1)
     du.start()
-    for step in sq.order()[2:]:
-        sq.along_z(step)
+    sq.along_z(Z - 1)
     do.start()
     dq.start()
     total = r.vg[1]
@@ -857,8 +955,11 @@
         arrive(r.vt.at[step - 1], vti[step - 1])
         total = total + r.vt[step - 1]
     r.gv[...] = total
-    for one in sent:
-        one.wait_send()
+    for one, only in sent:
+        if only is None:
+            one.wait_send()
+        else:
+            pl.when(only)(one.wait_send)
 
 
 def block_step(m, args):
@@ -890,6 +991,77 @@
             collective_id=0, has_side_effects=True, vmem_limit_bytes=62 * 1024 * 1024
         ),
         name="block_step",
+    )(*args)
+
+
+def update_kernel(pieces, passed, *refs):
+    count = len(pieces)
+    ins, outs = refs[: 3 * count + passed], refs[3 * count + passed :]
+    for k, parts in enumerate(pieces):
+        grad, master, moments = ins[3 * k : 3 * k + 3]
+        new, state, low = outs[3 * k : 3 * k + 3]
+        rows = min(16, master.shape[0])
+
+        def one(i, parts=parts, grad=grad, master=master, moments=moments, new=new, state=state, low=low, rows=rows):
+            own = pl.ds(pl.multiple_of(i * rows, rows), rows)
+            for block, source, column, width in parts:
+                cols = pl.ds(column, width)
+                value = grad[block, own, pl.ds(source, width)].astype(F32)
+                first = MOMENT_DECAY * moments[0, own, cols] + (1.0 - MOMENT_DECAY) * value
+                second = MOMENT_DECAY * moments[1, own, cols] + (1.0 - MOMENT_DECAY) * value * value
+                correction = 1.0 - MOMENT_DECAY**STEP
+                scaled = first / correction / (jnp.sqrt(second / correction) + ADAM_EPSILON)
+                old = master[own, cols]
+                updated = old - RATE_MATRIX * (scaled + WEIGHT_DECAY * old)
+                new[own, cols] = updated
+                state[0, own, cols] = first
+                state[1, own, cols] = second
+                low[own, cols] = updated.astype(BF)
+
+        loop(master.shape[0] // rows, one)
+    for source, target in zip(ins[3 * count :], outs[3 * count :]):
+        target[...] = source[...]
+
+
+def update_step(m, grads, masters, moments, passed):
+    pieces = [
+        [(t, b * m.Q, b * D + t * m.Q, m.Q) for b in range(3) for t in range(m.T)],
+        [(t, 0, t * m.Q, m.Q) for t in range(m.T)],
+        [(t, k * m.FD, (k * m.T + t) * m.FD, m.FD) for t in range(m.T) for k in range(m.W)],
+        [(0, k * 256, k * 256, 256) for k in range(D // 256)],
+    ]
+    if m.FD % 128:
+        pieces[2] = [(0, k * 256, k * 256, 256) for k in range(FF // 256)]
+    steps = 2 if m.RD % 32 == 0 else 1
+    args, specs, outs, out_specs = [], [], [], []
+
+    def spec(shape):
+        axis = len(shape) - 2
+        block = tuple(s // steps if k == axis else s for k, s in enumerate(shape))
+        return pl.BlockSpec(block, lambda i: tuple(i if k == axis else 0 for k in range(axis + 2)))
+
+    for grad, master, moment in zip(grads, masters, moments):
+        args += [grad, master, moment]
+        specs += [spec(a.shape) for a in (grad, master, moment)]
+        for shape, kind in ((master.shape, F32), (moment.shape, F32), (master.shape, BF)):
+            outs.append(jax.ShapeDtypeStruct(shape, kind))
+            out_specs.append(spec(shape))
+    for one in passed:
+        args.append(one)
+        specs.append(spec(one.shape))
+        outs.append(jax.ShapeDtypeStruct(one.shape, one.dtype))
+        out_specs.append(spec(one.shape))
+
+    def kernel(*refs):
+        update_kernel(pieces, len(passed), *refs)
+
+    return pl.pallas_call(
+        kernel,
+        grid=(steps,),
+        out_shape=outs,
+        in_specs=specs,
+        out_specs=out_specs,
+        name="update_step",
     )(*args)
 
 
@@ -936,24 +1108,23 @@
         gq, go, gu = [
             lax.all_to_all(g.reshape(m.T, m.RD, g.shape[1]), "narrow", 0, 0) for g in (gq, go, gu)
         ]
-    grad_qkv = gq.reshape(m.T, m.RD, 3, m.Q).transpose(1, 2, 0, 3).reshape(m.RD, 3 * D)
-    grad_out = go.transpose(1, 0, 2).reshape(m.RD, D)
-    grad_up = gu.reshape(m.T, m.RD, m.W, m.FD).transpose(1, 2, 0, 3).reshape(m.RD, FF)
+    if m.FD % 128:
+        gu = gu.reshape(m.T, m.RD, m.W, m.FD).transpose(1, 2, 0, 3).reshape(1, m.RD, FF)
     rise = gv[8 : 8 + m.T, : m.F].reshape(m.T, m.W, m.FD).transpose(1, 0, 2).reshape(FF // D, D)
     grad_vec = lax.dynamic_slice(
         jnp.concatenate([gv[:8], rise], axis=0), (0, first_row), (12, m.RD)
     ).T
 
-    new_qkv, state_qkv, copy_qkv = adam_update(
-        w_qkv, moments_qkv, grad_qkv.astype(F32), RATE_MATRIX, WEIGHT_DECAY
+    results = update_step(
+        m,
+        (gq, go, gu, gd.reshape(1, m.FD, D)),
+        (w_qkv, w_out, w_up, w_down),
+        (moments_qkv, moments_out, moments_up, moments_down),
+        (block_out, input_grad),
     )
-    new_out, state_out, copy_out = adam_update(
-        w_out, moments_out, grad_out.astype(F32), RATE_MATRIX, WEIGHT_DECAY
-    )
-    new_up, state_up, copy_up = adam_update(
-        w_up, moments_up, grad_up.astype(F32), RATE_MATRIX, WEIGHT_DECAY
-    )
-    new_down, state_down, copy_down = adam_update(w_down, moments_down, gd, RATE_MATRIX, WEIGHT_DECAY)
+    new_qkv, state_qkv, copy_qkv, new_out, state_out, copy_out = results[:6]
+    new_up, state_up, copy_up, new_down, state_down, copy_down = results[6:12]
+    block_out, input_grad = results[12:]
     new_vectors, state_vectors, copy_vectors = adam_update(
         vectors, moments_vec, grad_vec, RATE_VECTOR, 0.0
     )

time: 230 us -> 190 us (0.83)
  Pallas kernels: 199 us -> 178 us
  other arithmetic: 14.4 us -> 3.54 us
  local copies, waits for them, and re-layouts: 14.8 us -> 7.44 us
    pallas_call x1, Pallas kernels: 199 us -> 173 us  [block_step(): pl.pallas_call(kernel, out_shape=[jax.ShapeDtypeStruct((m.S, D), BF), jax...]
    unnamed x47 -> x14, local copies, waits for them, and re-layouts: 8.58 us -> 2.26 us
    another operation x7 -> x2, other arithmetic: 6.11 us -> 0.01 us  [adam_update(): jnp.stack([first_moment, second_moment])]
    pallas_call x0 -> x1, Pallas kernels: none -> 5.29 us  [update_step(): pl.pallas_call(kernel, grid=(steps,), out_shape=outs, in_specs=specs, out...]
    convert_element_type x4 -> x1, other arithmetic: 4.9 us -> 0.7 us  [adam_update(): updated.astype(BF)]
    convert_element_type x11 -> x0, local copies, waits for them, and re-layouts: 2.63 us -> none  [the longest x4 1.59 us: body(): grad_up.astype(F32)]
where the time goes in v3:
time: 190 us
  Pallas kernels  178 us (94%)
  local copies, waits for them, and re-layouts  7.44 us (4%)
  other arithmetic  3.54 us (2%)
    pallas_call x1, Pallas kernels, block_step(): pl.pallas_call(kernel, out_shape=[jax.ShapeDtypeStruct((m.S, D), BF), jax...  173 us
    pallas_call x1, Pallas kernels, update_step(): pl.pallas_call(kernel, grid=(steps,), out_shape=outs, in_specs=specs, out...  5.29 us

profile of v3, /device:TPU:0, one launch (start us, length us, event | category | flops | bytes accessed | tf_op | source)
XLA Modules:
  0.0 189.7 jit_solution(10193571015770713498)
XLA Ops:
  0.7 0.0 copy-start.3
  0.7 0.0 copy-start.2
  0.7 0.7 convert_bitcast_fusion.1
  1.4 0.6 broadcast_in_dim.11.refs_2_
  2.0 0.7 convert_bitcast_fusion
  2.7 0.8 fusion.11
  3.5 0.2 dynamic_update_slice.3
  3.8 0.6 fusion.1.refs_7_
  4.4 0.0 copy-done.3
  4.4 0.6 copy.78
  5.0 0.0 copy-done.2
  5.1 0.1 reshape.68
  5.2 0.0 copy-start
  5.2 0.1 copy.77
  5.3 0.9 reshape.69.refs_3_
  6.2 0.0 copy-done
  6.3 0.2 reshape.71
  6.4 0.0 copy-start.1
  6.5 0.8 reshape.72.refs_5_
  7.3 0.2 copy-done.1
  7.5 0.7 convert_element_type.27.refs_6_
  8.2 172.7 %block_step.1 = (bf16[128,1024]{1,0:T(8,128)(2,1)}, f32[128,1024]{1,0:T(8,128)}, bf16[4,32,768]{2,1,0:T(8,128)(2,1)}, bf16[4,32,256]{2,1,0:T(8,128)(2,1)}, bf16[...) custom-call(bf16[128,1024]{1,0:T(8,128)(2,1)} %refs_0_.1, bf16[128,1024]{1,0:T(8,128)(2,1)} %refs_1_.2, ...), custom_call_target="tpu_custom_call" | custom-call | tf_op jit(solution)/shard_map/block_step/pallas_call | solution.py:977
  180.9 0.8 slice_bitcast_fusion
  181.6 0.8 slice.21
  182.4 0.0 copy-start.4
  182.4 0.7 copy-done.4
  183.1 0.7 fusion.9
  183.8 0.6 copy.44
  184.4 5.3 %update_step.1 = (f32[32,3072]{1,0:T(8,128)}, f32[2,32,3072]{2,1,0:T(8,128)}, bf16[32,3072]{1,0:T(8,128)(2,1)}, f32[32,1024]{1,0:T(8,128)}, f32[2,32,1024]{2,1,0...) custom-call(bf16[4,32,768]{2,1,0:T(8,128)(2,1)} %get-tuple-element.3, ...), custom_call_target="tpu_custom_call" | custom-call | tf_op jit(solution)/shard_map/update_step/pallas_call | solution.py:1058
  (15 shorter events, 0.2 us)
Async XLA Ops:
  0.7 3.7 %copy-start.3 = (f32[32,1024]{1,0:T(8,128)S(1)}, f32[32,1024]{1,0:T(8,128)}, u32[]{:S(2)}) copy-start(f32[32,1024]{1,0:T(8,128)} %refs_4_.1) | copy-start | bytes 393220
  0.7 4.4 %copy-start.2 = (f32[32,3072]{1,0:T(8,128)S(1)}, f32[32,3072]{1,0:T(8,128)}, u32[]{:S(2)}) copy-start(f32[32,3072]{1,0:T(8,128)} %refs_1_.3) | copy-start | bytes 1179652
  5.2 1.0 copy-start
  6.4 1.0 copy-start.1
  182.4 0.7 copy-start.4

commit v4 on v3

--- a/solution.py
+++ b/solution.py
@@ -128,6 +128,9 @@
     out.update(scatter("u", m.RG, m.F))
     out.update(scatter("d", m.FD, D))
     if m.inside:
+        out["pq"] = ((m.T, m.RD, m.NQ), BF)
+        out["po"] = ((m.T, m.RD, m.Q), BF)
+        out["pu"] = ((m.T, m.RD, m.F), BF)
         out.update(spread("q", m.NQ))
         out.update(spread("o", m.Q))
         out.update(spread("u", m.F))
@@ -159,10 +162,18 @@
     out["dof"] = ((m.L, m.Q), BF)
     out["daq"] = ((m.L, m.Q), BF)
     out["sums"] = ((6, 16, D), F32)
+    out["bo"] = ((m.S, D), BF)
+    out["ig"] = ((m.S, D), F32)
+    out["gq"] = ((m.T, m.RD, m.NQ) if m.inside else (m.RG, m.NQ), BF)
+    out["go"] = ((m.T, m.RD, m.Q) if m.inside else (m.RG, m.Q), BF)
+    out["gu"] = ((m.T, m.RD, m.F) if m.inside else (m.RG, m.F), BF)
+    out["gd"] = ((m.FD, D), F32)
+    out["gv"] = ((16, D), F32)
     out["vg"] = ((3, 16, D), F32)
-    out["vx"] = ((m.X - 1, 16, D), F32)
-    out["vz"] = ((m.Z - 1, 16, D), F32)
-    out["vt"] = ((m.T - 1, 16, D), F32)
+    out["vb"] = ((3, 16, D), BF)
+    out["vx"] = ((m.X - 1, 16, D), BF)
+    out["vz"] = ((m.Z - 1, 16, D), BF)
+    out["vt"] = ((m.T - 1, 16, D), BF)
     return out
 
 
@@ -177,8 +188,16 @@
 
 def block_kernel(m, names, *refs):
     inputs = ("x", "dy", "seg", "pq", "po", "pu", "pd", "pv")
+    if m.inside:
+        inputs = ("x", "dy", "seg", "fq", "fo", "fu", "fd", "pv")
     outputs = ("bo", "ig", "gq", "go", "gu", "gd", "gv")
-    r = types.SimpleNamespace(**dict(zip(inputs + outputs + tuple(names) + ("sem",), refs)))
+    homes = tuple("h" + name for name in outputs)
+    r = types.SimpleNamespace(**dict(zip(inputs + homes + tuple(names) + ("sem", "done"), refs)))
+
+    def put(name):
+        k = outputs.index(name)
+        return pltpu.make_async_copy(getattr(r, name), getattr(r, "h" + name), r.done.at[k])
+
     w, n = lax.axis_index("wide"), lax.axis_index("narrow")
     z, x = w // m.X, lax.rem(w, m.X)
     y, c = n // 2, lax.rem(n, 2)
@@ -213,6 +232,14 @@
         else:
             pl.when(only)(one.start)
         sent.append((one, only))
+
+    def drain(count):
+        for one, only in sent[:count]:
+            if only is None:
+                one.wait_send()
+            else:
+                pl.when(only)(one.wait_send)
+        del sent[:count]
 
     def arrive(dst, index):
         copy(dst, dst, sibling, index).wait_recv()
@@ -517,10 +544,19 @@
     def transpose(target, source, count_rows, count_cols):
         def tile(k):
             i, j = k // count_cols, lax.rem(k, count_cols)
-            value = source(rows_of(i, 128), rows_of(j, 128)).astype(F32)
-            target[rows_of(j, 128), rows_of(i, 128)] = value.T.astype(BF)
+            target[rows_of(j, 128), rows_of(i, 128)] = source(rows_of(i, 128), rows_of(j, 128)).T
 
         loop(count_rows * count_cols, tile)
+
+    if m.inside:
+        for k in range(T):
+            r.po[k] = r.fo[:, k * m.Q : (k + 1) * m.Q].astype(BF)
+            for b in range(3):
+                first = b * D + k * m.Q
+                r.pq[k, :, b * m.Q : (b + 1) * m.Q] = r.fq[:, first : first + m.Q].astype(BF)
+            for j in range(m.W):
+                first = (j * T + k) * m.FD
+                r.pu[k, :, j * m.FD : (j + 1) * m.FD] = r.fu[:, first : first + m.FD].astype(BF)
 
     barrier = pltpu.get_barrier_semaphore()
     peers = [(w, up_n(k)) for k in range(1, T)]
@@ -544,7 +580,7 @@
     vi, si = fresh(T - 1), fresh(T - 1)
     for step in range(1, T):
         send(r.pv, r.vn.at[step - 1], (w, up_n(step)), vi[step - 1])
-    r.wd[w] = r.pd[...]
+    r.wd[w] = r.fd[...].astype(BF) if m.inside else r.pd[...]
     gd.forward(0)
 
     class Rows:
@@ -579,7 +615,7 @@
     own_rows = rows_of(n, S)
     r.tok[own_rows, :] = r.x[...]
     tokens.start()
-    r.sg[n] = r.seg[...]
+    r.sg[n] = jnp.broadcast_to(r.seg[...].astype(F32), (8, S))
     for step in range(1, T):
         send(r.sg.at[n], r.sg.at[n], (w, up_n(step)), si[step - 1])
     ru.start()
@@ -712,7 +748,6 @@
     seconds.start()
     gd.inside(early)
     gd.ends(range(1, 2))
-    seconds.middle()
     for t in range(T):
         for k in range(m.Q // 128):
             base = t * m.Q + k * 128
@@ -722,10 +757,10 @@
                 r.ot[base : base + 128, rows_of(i, 128)] = value.T.astype(BF)
 
             loop(L // 128, turn)
+    seconds.middle()
     seconds.close()
     gd.inside(late)
     gd.ends(range(2, Z - 1))
-    transpose(r.ct, lambda i, j: r.ca[i, j], L // 128, D // 128)
     gd.ends(late)
     gu.finish()
 
@@ -750,8 +785,10 @@
     for step in sd.order()[1:]:
         sd.multiply(step, r.ht, r.dya)
         sd.along_x(step)
-    sd.along_z(sd.order()[0])
+    transpose(r.ct, lambda i, j: r.ca[i, j], L // 128, D // 128)
+    sd.along_z(0)
     gd.finish()
+    early_sends = len(sent)
 
     group = 256 // m.FD
 
@@ -858,13 +895,11 @@
     tin.start()
     for step in range(1, T):
         arrive(r.daq.at[rows_of(down_n(step), S)], ai[step - 1])
-    for step in so.order():
-        so.multiply(step, r.ot, r.daq)
-        so.along_x(step)
     tin.middle()
     su.along_z(1)
     for step in sq.order():
         sq.multiply(step, r.at, r.dqkv)
+        sq.along_x(step)
     for step in su.order()[2:-1]:
         su.along_z(step)
     su.join(0)
@@ -894,14 +929,17 @@
         r.sums[1] += grad
 
     loop(S // 16, first_back)
+    put("ig").start()
     r.vg[0, 0:1, :] = jnp.sum(r.sums[0], axis=0, keepdims=True)
     r.vg[0, 1:2, :] = jnp.sum(r.sums[1], axis=0, keepdims=True)
+    r.vb[0] = r.vg[0].astype(BF)
     vxi, vzi, vti = fresh(X - 1), fresh(Z - 1), fresh(T - 1)
     for dx in range(1, X):
-        send(r.vg.at[0], r.vx.at[dx - 1], (z * X + up_x(dx), n), vxi[dx - 1])
-
-    for step in sq.order():
-        sq.along_x(step)
+        send(r.vb.at[0], r.vx.at[dx - 1], (z * X + up_x(dx), n), vxi[dx - 1])
+
+    for step in so.order():
+        so.multiply(step, r.ot, r.daq)
+        so.along_x(step)
     su.join(1)
     su.along_z(su.order()[-1])
     ty.finish()
@@ -911,17 +949,8 @@
         r.bo[rows, :] = (r.r1[rows, :] + ty.rows(rows) + r.vec[7:8, :]).astype(BF)
 
     loop(S // 16, close)
-    for step in so.order():
-        so.along_z(step)
-    so.join(0)
-    so.join(1)
-    total = r.vg[0]
-    for dx in range(1, X):
-        arrive(r.vx.at[dx - 1], vxi[dx - 1])
-        total = total + r.vx[dx - 1]
-    r.vg[1] = total
-    for step in range(1, Z):
-        send(r.vg.at[1], r.vz.at[step - 1], (up_z(step) * X + x, n), vzi[step - 1])
+    put("bo").start()
+    drain(early_sends)
     sd.finish()
 
     def keep(i):
@@ -929,6 +958,7 @@
         r.gd[rows, :] = sd.total(rows)
 
     loop(m.FD // 16, keep)
+    put("gd").start()
     du, do, dq = Deal("u", su, r.gu), Deal("o", so, r.go), Deal("q", sq, r.gq)
     for step in sq.order()[:2]:
         sq.along_z(step)
@@ -938,28 +968,44 @@
     sq.join(1)
     du.start()
     sq.along_z(Z - 1)
+    for step in so.order()[:-1]:
+        so.along_z(step)
+    so.join(0)
+    so.join(1)
+    so.along_z(Z - 1)
+    total = r.vg[0]
+    for dx in range(1, X):
+        arrive(r.vx.at[dx - 1], vxi[dx - 1])
+        total = total + r.vx[dx - 1].astype(F32)
+    r.vg[1] = total
+    r.vb[1] = total.astype(BF)
+    for step in range(1, Z):
+        send(r.vb.at[1], r.vz.at[step - 1], (up_z(step) * X + x, n), vzi[step - 1])
+    dq.start()
     do.start()
-    dq.start()
     total = r.vg[1]
     for step in range(1, Z):
         arrive(r.vz.at[step - 1], vzi[step - 1])
-        total = total + r.vz[step - 1]
+        total = total + r.vz[step - 1].astype(F32)
     r.vg[2] = total
+    r.vb[2] = total.astype(BF)
     for step in range(1, T):
-        send(r.vg.at[2], r.vt.at[step - 1], (w, up_n(step)), vti[step - 1])
+        send(r.vb.at[2], r.vt.at[step - 1], (w, up_n(step)), vti[step - 1])
     du.finish()
+    put("gu").start()
+    dq.finish()
+    put("gq").start()
     do.finish()
-    dq.finish()
+    put("go").start()
     total = r.vg[2]
     for step in range(1, T):
         arrive(r.vt.at[step - 1], vti[step - 1])
-        total = total + r.vt[step - 1]
+        total = total + r.vt[step - 1].astype(F32)
     r.gv[...] = total
-    for one, only in sent:
-        if only is None:
-            one.wait_send()
-        else:
-            pl.when(only)(one.wait_send)
+    put("gv").start()
+    drain(len(sent))
+    for name in outputs:
+        put(name).wait()
 
 
 def block_step(m, args):
@@ -984,9 +1030,9 @@
             jax.ShapeDtypeStruct((16, D), F32),
         ],
         in_specs=[vmem] * len(args),
-        out_specs=[vmem] * 7,
+        out_specs=[pl.BlockSpec(memory_space=pl.ANY)] * 7,
         scratch_shapes=[pltpu.VMEM(shape, kind) for shape, kind in scratch.values()]
-        + [pltpu.SemaphoreType.DMA((semaphores_of(m),))],
+        + [pltpu.SemaphoreType.DMA((semaphores_of(m),)), pltpu.SemaphoreType.DMA((7,))],
         compiler_params=pltpu.CompilerParams(
             collective_id=0, has_side_effects=True, vmem_limit_bytes=62 * 1024 * 1024
         ),
@@ -1085,24 +1131,25 @@
     device = lax.axis_index("wide") * narrow + lax.axis_index("narrow")
     first_row = device * m.RD
 
-    pq = w_qkv.astype(BF).reshape(m.RD, 3, m.T, m.Q).transpose(2, 0, 1, 3)
-    po = w_out.astype(BF).reshape(m.RD, m.T, m.Q).transpose(1, 0, 2)
-    pu = w_up.astype(BF).reshape(m.RD, m.W, m.T, m.FD).transpose(2, 0, 1, 3)
-    parts = [pq.reshape(m.T, m.RD, m.NQ), po, pu.reshape(m.T, m.RD, m.F)]
+    parts = [w_qkv, w_out, w_up, w_down]
     if not m.inside:
+        pq = w_qkv.astype(BF).reshape(m.RD, 3, m.T, m.Q).transpose(2, 0, 1, 3)
+        po = w_out.astype(BF).reshape(m.RD, m.T, m.Q).transpose(1, 0, 2)
+        pu = w_up.astype(BF).reshape(m.RD, m.W, m.T, m.FD).transpose(2, 0, 1, 3)
+        parts = [pq.reshape(m.T, m.RD, m.NQ), po, pu.reshape(m.T, m.RD, m.F)]
         parts = [
             lax.all_to_all(part, "narrow", 0, 0).reshape(m.RG, part.shape[2]) for part in parts
         ]
+        parts.append(w_down.astype(BF))
     low = vectors.astype(BF).T
     spot = jnp.zeros((12, D), BF)
     spot = lax.dynamic_update_slice(spot, low, (0, first_row))
     rise = spot[8:].reshape(m.W, m.T, m.FD).transpose(1, 0, 2).reshape(m.T, m.F)
     rise = jnp.pad(rise, ((0, 8 - m.T), (0, D - m.F)))
     packed = jnp.concatenate([spot[:8], rise], axis=0)
-    segments = jnp.broadcast_to(segment_ids.astype(F32), (8, m.S))
 
     block_out, input_grad, gq, go, gu, gd, gv = block_step(
-        m, (tokens, cotangent, segments, *parts, w_down.astype(BF), packed)
+        m, (tokens, cotangent, segment_ids, *parts, packed)
     )
     if not m.inside:
         gq, go, gu = [

time: 190 us -> 178 us (0.937)
  Pallas kernels: 178 us -> 172 us
  local copies, waits for them, and re-layouts: 7.44 us -> 3.09 us
  other arithmetic: 3.54 us -> 1.34 us
    pallas_call x1, Pallas kernels: 173 us -> 167 us  [block_step(): pl.pallas_call(kernel, out_shape=[jax.ShapeDtypeStruct((m.S, D), BF), jax...]
    reshape x7 -> x0, local copies, waits for them, and re-layouts: 2.79 us -> none  [the longest x2 1.72 us: body(): parts = [pq.reshape(m.T, m.RD, m.NQ), po, pu.reshape(m.T, m.RD, m.F)]]
where the time goes in v4:
time: 178 us; the launch traced here: 177 us
  Pallas kernels  172 us (97%)
  local copies, waits for them, and re-layouts  3.09 us (2%)
    pallas_call x1, Pallas kernels, block_step(): pl.pallas_call(kernel, out_shape=[jax.ShapeDtypeStruct((m.S, D), BF), jax...  167 us
    pallas_call x1, Pallas kernels, update_step(): pl.pallas_call(kernel, grid=(steps,), out_shape=outs, in_specs=specs, out...  5.29 us

profile of v4, /device:TPU:0, one launch (start us, length us, event | category | flops | bytes accessed | tf_op | source)
XLA Modules:
  0.0 177.5 jit_solution(17020253966538575178)
XLA Ops:
  0.7 0.0 copy-start
  0.7 0.0 copy-start.1
  0.7 0.7 copy-done
  1.4 0.0 copy-done.1
  1.4 0.2 dynamic_update_slice.3
  1.7 0.6 fusion.1.refs_7_
  2.3 167.0 %block_step.1 = (bf16[128,1024]{1,0:T(8,128)(2,1)}, f32[128,1024]{1,0:T(8,128)}, bf16[4,32,768]{2,1,0:T(8,128)(2,1)}, bf16[4,32,256]{2,1,0:T(8,128)(2,1)}, bf16[...) custom-call(bf16[128,1024]{1,0:T(8,128)(2,1)} %refs_0_.1, bf16[128,1024]{1,0:T(8,128)(2,1)} %refs_1_.2, ...), custom_call_target="tpu_custom_call" | custom-call | tf_op jit(solution)/shard_map/block_step/pallas_call | solution.py:1023
  169.3 0.8 slice_bitcast_fusion
  170.1 0.8 slice.21
  170.9 0.7 fusion.9
  171.6 0.6 copy.34
  172.2 5.3 %update_step.1 = (f32[32,3072]{1,0:T(8,128)}, f32[2,32,3072]{2,1,0:T(8,128)}, bf16[32,3072]{1,0:T(8,128)(2,1)}, f32[32,1024]{1,0:T(8,128)}, f32[2,32,1024]{2,1,0...) custom-call(bf16[4,32,768]{2,1,0:T(8,128)(2,1)} %get-tuple-element.3, ...), custom_call_target="tpu_custom_call" | custom-call | tf_op jit(solution)/shard_map/update_step/pallas_call | solution.py:1104
  (13 shorter events, 0.1 us)
Async XLA Ops:
  0.7 0.7 copy-start
  0.7 0.7 copy-start.1

commit v5 on v4

--- a/solution.py
+++ b/solution.py
@@ -84,6 +84,8 @@
     m.NH = m.Q // HEAD
     m.inside = m.RD % 16 == 0
     m.line = m.Z == 4
+    m.compact = m.inside and m.RG == 128 and m.FD == 128
+    m.V = m.RG if m.compact else D
     return m
 
 
@@ -121,8 +123,8 @@
     out["wo"] = ((m.T, m.W, m.RG, m.Q), BF)
     out.update(weights("wu", m.RG, m.F))
     out.update(weights("wd", m.FD, D))
-    out.update(weights("wv", 16, D))
-    out["vn"] = ((m.T - 1, 16, D), BF)
+    out.update(weights("wv", 16, m.V))
+    out["vn"] = ((m.T - 1, 16, m.V), BF)
     out.update(scatter("q", m.RG, m.NQ))
     out.update(scatter("o", m.RG, m.Q))
     out.update(scatter("u", m.RG, m.F))
@@ -168,7 +170,7 @@
     out["go"] = ((m.T, m.RD, m.Q) if m.inside else (m.RG, m.Q), BF)
     out["gu"] = ((m.T, m.RD, m.F) if m.inside else (m.RG, m.F), BF)
     out["gd"] = ((m.FD, D), F32)
-    out["gv"] = ((16, D), F32)
+    out["gv"] = ((16, m.V), F32)
     out["vg"] = ((3, 16, D), F32)
     out["vb"] = ((3, 16, D), BF)
     out["vx"] = ((m.X - 1, 16, D), BF)
@@ -644,10 +646,18 @@
     gv.ends(range(1, Z))
     tokens.close()
     gv.finish()
-    vector = r.wv[0].astype(F32)
-    for k in range(1, m.W):
-        vector = vector + r.wv[k].astype(F32)
-    r.vec[...] = vector
+    if m.compact:
+        for k in range(m.W):
+            vector = r.wv[k].astype(F32)
+            r.vec[0:8, k * m.V : (k + 1) * m.V] = vector[0:8]
+            for part in range(FF // D):
+                first = (part * (D // (T * m.FD)) + k // T) * m.FD
+                r.vec[8 + k % T : 9 + k % T, first : first + m.FD] = vector[8 + part : 9 + part]
+    else:
+        vector = r.wv[0].astype(F32)
+        for k in range(1, m.W):
+            vector = vector + r.wv[k].astype(F32)
+        r.vec[...] = vector
 
     heads = rows_of(n, m.Q)
     r.bias[...] = jnp.zeros_like(r.bias)
@@ -728,6 +738,7 @@
     gu.ends(range(2, Z - 1))
     outs.close()
     mixes.middle()
+    gd.inside(early)
     gu.ends(late)
     mixes.close()
 
@@ -746,7 +757,6 @@
 
     loop(S // 16, second_norm)
     seconds.start()
-    gd.inside(early)
     gd.ends(range(1, 2))
     for t in range(T):
         for k in range(m.Q // 128):
@@ -761,7 +771,6 @@
     seconds.close()
     gd.inside(late)
     gd.ends(range(2, Z - 1))
-    gd.ends(late)
     gu.finish()
 
     def expand(j):
@@ -779,6 +788,7 @@
         r.u[rows, :] = phi + value * (jnp.exp(-0.5 * value * value) * 0.3989422804014327)
 
     loop(L // 16, activate)
+    gd.ends(late)
     transpose(r.ht, lambda i, j: r.h[i, j], L // 128, m.F // 128)
     sd.multiply(sd.order()[0], r.ht, r.dya)
     sd.along_x(sd.order()[0])
@@ -1001,7 +1011,18 @@
     for step in range(1, T):
         arrive(r.vt.at[step - 1], vti[step - 1])
         total = total + r.vt[step - 1].astype(F32)
-    r.gv[...] = total
+    if m.compact:
+        r.vg[0] = total
+        r.gv[...] = jnp.zeros_like(r.gv)
+        r.gv[0:8, :] = r.vg[0, 0:8, rows_of(w, m.V)]
+        for part in range(FF // D):
+            block = part * (D // (T * m.FD)) + w // T
+            several = r.vg[0, 8:16, rows_of(block, m.FD)]
+            row = lax.broadcasted_iota(jnp.int32, several.shape, 0)
+            mine = jnp.where(row == lax.rem(w, T), several, 0.0)
+            r.gv[8 + part : 9 + part, :] = jnp.sum(mine, axis=0, keepdims=True)
+    else:
+        r.gv[...] = total
     put("gv").start()
     drain(len(sent))
     for name in outputs:
@@ -1027,7 +1048,7 @@
             jax.ShapeDtypeStruct((m.S, D), F32),
             *grads,
             jax.ShapeDtypeStruct((m.FD, D), F32),
-            jax.ShapeDtypeStruct((16, D), F32),
+            jax.ShapeDtypeStruct((16, m.V), F32),
         ],
         in_specs=[vmem] * len(args),
         out_specs=[pl.BlockSpec(memory_space=pl.ANY)] * 7,
@@ -1142,11 +1163,13 @@
         ]
         parts.append(w_down.astype(BF))
     low = vectors.astype(BF).T
-    spot = jnp.zeros((12, D), BF)
-    spot = lax.dynamic_update_slice(spot, low, (0, first_row))
-    rise = spot[8:].reshape(m.W, m.T, m.FD).transpose(1, 0, 2).reshape(m.T, m.F)
-    rise = jnp.pad(rise, ((0, 8 - m.T), (0, D - m.F)))
-    packed = jnp.concatenate([spot[:8], rise], axis=0)
+    place = lax.axis_index("narrow") * m.RD if m.compact else first_row
+    spot = lax.dynamic_update_slice(jnp.zeros((16, m.V), BF), low, (0, place))
+    packed = spot
+    if not m.compact:
+        rise = spot[8:12].reshape(m.W, m.T, m.FD).transpose(1, 0, 2).reshape(m.T, m.F)
+        rise = jnp.pad(rise, ((0, 8 - m.T), (0, D - m.F)))
+        packed = jnp.concatenate([spot[:8], rise], axis=0)
 
     block_out, input_grad, gq, go, gu, gd, gv = block_step(
         m, (tokens, cotangent, segment_ids, *parts, packed)
@@ -1157,10 +1180,10 @@
         ]
     if m.FD % 128:
         gu = gu.reshape(m.T, m.RD, m.W, m.FD).transpose(1, 2, 0, 3).reshape(1, m.RD, FF)
-    rise = gv[8 : 8 + m.T, : m.F].reshape(m.T, m.W, m.FD).transpose(1, 0, 2).reshape(FF // D, D)
-    grad_vec = lax.dynamic_slice(
-        jnp.concatenate([gv[:8], rise], axis=0), (0, first_row), (12, m.RD)
-    ).T
+    if not m.compact:
+        rise = gv[8 : 8 + m.T, : m.F].reshape(m.T, m.W, m.FD).transpose(1, 0, 2).reshape(FF // D, D)
+        gv = jnp.concatenate([gv[:8], rise], axis=0)
+    grad_vec = lax.dynamic_slice(gv, (0, place), (12, m.RD)).T
 
     results = update_step(
         m,

time: 178 us -> 175 us (0.983)
  Pallas kernels: 172 us -> 169 us
    pallas_call x1, Pallas kernels: 167 us -> 164 us  [block_step(): pl.pallas_call(kernel, out_shape=[jax.ShapeDtypeStruct((m.S, D), BF), jax...]
where the time goes in v5:
time: 175 us; the launch traced here: 174 us
  Pallas kernels  169 us (97%)
  local copies, waits for them, and re-layouts  3.56 us (2%)
    pallas_call x1, Pallas kernels, block_step(): pl.pallas_call(kernel, out_shape=[jax.ShapeDtypeStruct((m.S, D), BF), jax...  164 us
    pallas_call x1, Pallas kernels, update_step(): pl.pallas_call(kernel, grid=(steps,), out_shape=outs, in_specs=specs, out...  5.32 us

profile of v5, /device:TPU:0, one launch (start us, length us, event | category | flops | bytes accessed | tf_op | source)
XLA Modules:
  0.0 174.4 jit_solution(9079250981721702026)
XLA Ops:
  0.7 0.0 copy-start
  0.7 0.7 copy-done
  1.4 0.3 dynamic_update_slice.3.refs_7_
  1.6 0.0 copy-start.1
  1.7 0.6 copy-done.1
  2.2 164.1 %block_step.1 = (bf16[128,1024]{1,0:T(8,128)(2,1)}, f32[128,1024]{1,0:T(8,128)}, bf16[4,32,768]{2,1,0:T(8,128)(2,1)}, bf16[4,32,256]{2,1,0:T(8,128)(2,1)}, bf16[...) custom-call(bf16[128,1024]{1,0:T(8,128)(2,1)} %refs_0_.1, bf16[128,1024]{1,0:T(8,128)(2,1)} %refs_1_.2, ...), custom_call_target="tpu_custom_call" | custom-call | tf_op jit(solution)/shard_map/block_step/pallas_call | solution.py:1044
  166.4 5.3 %update_step.1 = (f32[32,3072]{1,0:T(8,128)}, f32[2,32,3072]{2,1,0:T(8,128)}, bf16[32,3072]{1,0:T(8,128)(2,1)}, f32[32,1024]{1,0:T(8,128)}, f32[2,32,1024]{2,1,0...) custom-call(bf16[4,32,768]{2,1,0:T(8,128)(2,1)} %get-tuple-element.3, ...), custom_call_target="tpu_custom_call" | custom-call | tf_op jit(solution)/shard_map/update_step/pallas_call | solution.py:1125
  171.7 0.0 copy-start.2
  171.7 0.7 copy-done.2
  172.4 0.0 copy-start.3
  172.4 0.7 copy-done.3
  173.1 0.7 fusion.5
  173.8 0.6 copy.32
  (4 shorter events, 0.0 us)
Async XLA Ops:
  0.7 0.7 copy-start
  1.6 0.6 copy-start.1
  171.7 0.7 copy-start.2
  172.4 0.7 copy-start.3
